TPU v7x, 16 devices: a 4x2x1 block of a 4x4x8 slice. The times are simulated.
16 devices in a mesh: dp: 2 (over y, z), fsdp: 8 (over x, core).
Axes of the slice: x: 4, y: 2, z: 1, core: 2. Of those that a mesh axis runs over, the one named last changes fastest.
The devices are a block of a 4x4x8 slice.
Arguments:
- hidden: bfloat16 [16384, 512], P(('dp', 'fsdp')), parts along dimension 0
- targets: int32 [16384], P(('dp', 'fsdp')), parts along dimension 0
- weight: bfloat16 [32128, 512], P('fsdp')
Outputs:
- output 1: float32 [2], P('dp'), parts along dimension 0
- output 2: float32 [16384, 512], P(('dp', 'fsdp')), parts along dimension 0
- output 3: float32 [64256, 512], P(('dp', 'fsdp')), parts along dimension 0
There are 2 independent parts. A program takes and returns all parts, laid end to end along the dimension named above; an argument that names none is the same for every part.
All inputs are finite; a program needn't handle non-finite values.
Results may differ from a plain program's by a relative error of at most 0.001.
Values are sent between devices in bfloat16 or wider.
A program may use at most 768 MiB of HBM per device.

v0:
```python
import jax
import jax.numpy as jnp
from jax import lax
from jax.sharding import PartitionSpec as P


def solution(mesh):
    groups = mesh.shape["fsdp"]
    ring_pairs = [(src_idx, (src_idx + 1) % groups) for src_idx in range(groups)]
    tok_spec = P(("dp", "fsdp"), None)

    def local_head(hidden, targets, weight):
        tok_loc = hidden.shape[0]
        shard_rows = weight.shape[0]
        tokens = tok_loc * groups
        rank_id = lax.axis_index("fsdp")
        col_ids = jnp.arange(shard_rows, dtype=jnp.int32)

        def block_logits(w_blk, step_idx):
            owner_idx = (rank_id - step_idx) % groups
            logits = lax.dot_general(hidden, w_blk, (((1,), (1,)), ((), ())), preferred_element_type=jnp.float32)
            is_target = (targets - owner_idx * shard_rows)[:, None] == col_ids[None, :]
            return logits, is_target

        def fwd_update(fwd_state, w_blk, step_idx):
            run_max, run_sum, tgt_logit = fwd_state
            logits, is_target = block_logits(w_blk, step_idx)
            new_max = jnp.maximum(run_max, jnp.max(logits, axis=1))
            run_sum = run_sum * jnp.exp(run_max - new_max) + jnp.sum(jnp.exp(logits - new_max[:, None]), axis=1)
            tgt_logit = tgt_logit + jnp.sum(jnp.where(is_target, logits, 0.0), axis=1)
            return new_max, run_sum, tgt_logit

        def fwd_body(step_idx, loop_state):
            w_cur, fwd_state = loop_state
            w_cur = lax.ppermute(w_cur, "fsdp", ring_pairs)
            return w_cur, fwd_update(fwd_state, w_cur, step_idx)

        init_state = (jnp.full((tok_loc,), -jnp.inf, jnp.float32), jnp.zeros((tok_loc,), jnp.float32), jnp.zeros((tok_loc,), jnp.float32))
        first_state = fwd_update(init_state, weight, 0)
        run_max, run_sum, tgt_logit = lax.fori_loop(1, groups, fwd_body, (weight, first_state))[1]
        log_norm = run_max + jnp.log(run_sum)
        loss_val = lax.psum(jnp.sum(log_norm - tgt_logit) / tokens, "fsdp").reshape(1)

        def bwd_update(w_blk, step_idx):
            logits, is_target = block_logits(w_blk, step_idx)
            dlogits = ((jnp.exp(logits - log_norm[:, None]) - is_target.astype(jnp.float32)) / tokens).astype(jnp.bfloat16)
            dh_part = jnp.dot(dlogits, w_blk, preferred_element_type=jnp.float32)
            dw_part = lax.dot_general(dlogits, hidden, (((0,), (0,)), ((), ())), preferred_element_type=jnp.float32)
            return dh_part, dw_part

        def bwd_body(step_idx, loop_state):
            w_cur, dw_acc, grad_h = loop_state
            w_cur = lax.ppermute(w_cur, "fsdp", ring_pairs)
            dw_acc = lax.ppermute(dw_acc, "fsdp", ring_pairs)
            dh_part, dw_part = bwd_update(w_cur, step_idx)
            return w_cur, dw_acc + dw_part, grad_h + dh_part

        grad_h, dw_acc = bwd_update(weight, 0)
        final_state = lax.fori_loop(1, groups, bwd_body, (weight, dw_acc, grad_h))
        grad_w = lax.ppermute(final_state[1], "fsdp", ring_pairs)
        return loss_val, final_state[2], grad_w

    return jax.shard_map(local_head, mesh=mesh, in_specs=(tok_spec, P(("dp", "fsdp")), P("fsdp", None)), out_specs=(P("dp"), tok_spec, tok_spec), check_vma=False)
```

profile of v0, /device:TPU:113, one launch (start us, length us, event | category | flops | bytes accessed | tf_op | source)
XLA Modules:
  0.0 1754.6 jit_solution(15196520551793620087)
XLA Ops:
  9.7 8.0 fusion.7
  17.7 8.0 select_reduce_fusion.1
  25.7 435.9 %while.42 = (s32[]{:T(128)}, bf16[4016,512]{1,0:T(8,128)(2,1)}, f32[1024]{0:T(1024)S(1)}, f32[1024]{0:T(1024)S(1)}, f32[1024]{0:T(1024)S(1)}, /*index=5*/bf16[10...) while((s32[]{:T(128)}, bf16[4016,512]{1,0:T(8,128)(2,1)}, ...), condition=%wide.region_7.8_spmd.clone, body=%wide.region_3.7_spmd.clone.sunk | while | flops 4235758592 | bytes 62816552 | solution.py:40
  28.4 44.5 %collective-permute-done = bf16[4016,512]{1,0:T(8,128)(2,1)} collective-permute-done((bf16[4016,512]{1,0:T(8,128)(2,1)}, bf16[4016,512]{1,0:T(8,128)(2,1)}, u32[]{:S(2)}, u32[]{:S(2)}) %collective-permute-start) | collective-permute-done | bytes 4112416 | tf_op jit(solution)/shard_map/while/body/eval_jaxpr/ppermute | solution.py:35
  90.6 44.5 %collective-permute-done = bf16[4016,512]{1,0:T(8,128)(2,1)} collective-permute-done((bf16[4016,512]{1,0:T(8,128)(2,1)}, bf16[4016,512]{1,0:T(8,128)(2,1)}, u32[]{:S(2)}, u32[]{:S(2)}) %collective-permute-start) | collective-permute-done | bytes 4112416 | tf_op jit(solution)/shard_map/while/body/eval_jaxpr/ppermute | solution.py:35
  135.2 6.4 fusion.31
  152.9 44.5 %collective-permute-done = bf16[4016,512]{1,0:T(8,128)(2,1)} collective-permute-done((bf16[4016,512]{1,0:T(8,128)(2,1)}, bf16[4016,512]{1,0:T(8,128)(2,1)}, u32[]{:S(2)}, u32[]{:S(2)}) %collective-permute-start) | collective-permute-done | bytes 4112416 | tf_op jit(solution)/shard_map/while/body/eval_jaxpr/ppermute | solution.py:35
  197.4 6.4 fusion.31
  215.1 44.5 %collective-permute-done = bf16[4016,512]{1,0:T(8,128)(2,1)} collective-permute-done((bf16[4016,512]{1,0:T(8,128)(2,1)}, bf16[4016,512]{1,0:T(8,128)(2,1)}, u32[]{:S(2)}, u32[]{:S(2)}) %collective-permute-start) | collective-permute-done | bytes 4112416 | tf_op jit(solution)/shard_map/while/body/eval_jaxpr/ppermute | solution.py:35
  259.7 6.4 fusion.31
  277.4 44.5 %collective-permute-done = bf16[4016,512]{1,0:T(8,128)(2,1)} collective-permute-done((bf16[4016,512]{1,0:T(8,128)(2,1)}, bf16[4016,512]{1,0:T(8,128)(2,1)}, u32[]{:S(2)}, u32[]{:S(2)}) %collective-permute-start) | collective-permute-done | bytes 4112416 | tf_op jit(solution)/shard_map/while/body/eval_jaxpr/ppermute | solution.py:35
  321.9 6.4 fusion.31
  339.6 44.5 %collective-permute-done = bf16[4016,512]{1,0:T(8,128)(2,1)} collective-permute-done((bf16[4016,512]{1,0:T(8,128)(2,1)}, bf16[4016,512]{1,0:T(8,128)(2,1)}, u32[]{:S(2)}, u32[]{:S(2)}) %collective-permute-start) | collective-permute-done | bytes 4112416 | tf_op jit(solution)/shard_map/while/body/eval_jaxpr/ppermute | solution.py:35
  384.1 6.4 fusion.31
  401.8 44.5 %collective-permute-done = bf16[4016,512]{1,0:T(8,128)(2,1)} collective-permute-done((bf16[4016,512]{1,0:T(8,128)(2,1)}, bf16[4016,512]{1,0:T(8,128)(2,1)}, u32[]{:S(2)}, u32[]{:S(2)}) %collective-permute-start) | collective-permute-done | bytes 4112416 | tf_op jit(solution)/shard_map/while/body/eval_jaxpr/ppermute | solution.py:35
  462.2 9.5 fusion.4
  473.7 7.5 fusion.5
  481.2 1148.8 %while.43 = (s32[]{:T(128)}, bf16[4016,512]{1,0:T(8,128)(2,1)}, f32[4016,512]{1,0:T(8,128)}, f32[1024,512]{1,0:T(8,128)S(1)}, bf16[1024,512]{1,0:T(8,128)(2,1)S(...) while((s32[]{:T(128)}, bf16[4016,512]{1,0:T(8,128)(2,1)}, ...), condition=%wide.region_11.12_spmd.clone, body=%wide.region_10.11_spmd.clone.sunk | while | flops 12660499456 | bytes 113230160 | solution.py:59
  483.7 132.7 %collective-permute-done.1 = bf16[4016,512]{1,0:T(8,128)(2,1)} collective-permute-done((bf16[4016,512]{1,0:T(8,128)(2,1)}, bf16[4016,512]{1,0:T(8,128)(2,1)}, u32[]{:S(2)}, u32[]{:S(2)}) %collective-permute-start.1) | collective-permute-done | bytes 4112416 | tf_op jit(solution)/shard_map/while/body/eval_jaxpr/ppermute | solution.py:53
  620.7 9.2 multiply_convert_fusion.5
  630.0 6.5 convolution_add_fusion.5
  636.5 8.8 convolution_add_fusion.4
  647.8 132.7 %collective-permute-done.1 = bf16[4016,512]{1,0:T(8,128)(2,1)} collective-permute-done((bf16[4016,512]{1,0:T(8,128)(2,1)}, bf16[4016,512]{1,0:T(8,128)(2,1)}, u32[]{:S(2)}, u32[]{:S(2)}) %collective-permute-start.1) | collective-permute-done | bytes 4112416 | tf_op jit(solution)/shard_map/while/body/eval_jaxpr/ppermute | solution.py:53
  784.8 9.2 multiply_convert_fusion.5
  794.0 6.5 convolution_add_fusion.5
  800.6 8.8 convolution_add_fusion.4
  811.9 132.7 %collective-permute-done.1 = bf16[4016,512]{1,0:T(8,128)(2,1)} collective-permute-done((bf16[4016,512]{1,0:T(8,128)(2,1)}, bf16[4016,512]{1,0:T(8,128)(2,1)}, u32[]{:S(2)}, u32[]{:S(2)}) %collective-permute-start.1) | collective-permute-done | bytes 4112416 | tf_op jit(solution)/shard_map/while/body/eval_jaxpr/ppermute | solution.py:53
  948.9 9.2 multiply_convert_fusion.5
  958.2 6.5 convolution_add_fusion.5
  964.7 8.8 convolution_add_fusion.4
  976.0 132.7 %collective-permute-done.1 = bf16[4016,512]{1,0:T(8,128)(2,1)} collective-permute-done((bf16[4016,512]{1,0:T(8,128)(2,1)}, bf16[4016,512]{1,0:T(8,128)(2,1)}, u32[]{:S(2)}, u32[]{:S(2)}) %collective-permute-start.1) | collective-permute-done | bytes 4112416 | tf_op jit(solution)/shard_map/while/body/eval_jaxpr/ppermute | solution.py:53
  1113.0 9.2 multiply_convert_fusion.5
  1122.3 6.5 convolution_add_fusion.5
  1128.8 8.8 convolution_add_fusion.4
  1140.1 132.7 %collective-permute-done.1 = bf16[4016,512]{1,0:T(8,128)(2,1)} collective-permute-done((bf16[4016,512]{1,0:T(8,128)(2,1)}, bf16[4016,512]{1,0:T(8,128)(2,1)}, u32[]{:S(2)}, u32[]{:S(2)}) %collective-permute-start.1) | collective-permute-done | bytes 4112416 | tf_op jit(solution)/shard_map/while/body/eval_jaxpr/ppermute | solution.py:53
  1277.1 9.2 multiply_convert_fusion.5
  1286.4 6.5 convolution_add_fusion.5
  1292.9 8.8 convolution_add_fusion.4
  1304.2 132.7 %collective-permute-done.1 = bf16[4016,512]{1,0:T(8,128)(2,1)} collective-permute-done((bf16[4016,512]{1,0:T(8,128)(2,1)}, bf16[4016,512]{1,0:T(8,128)(2,1)}, u32[]{:S(2)}, u32[]{:S(2)}) %collective-permute-start.1) | collective-permute-done | bytes 4112416 | tf_op jit(solution)/shard_map/while/body/eval_jaxpr/ppermute | solution.py:53
  1441.2 9.2 multiply_convert_fusion.5
  1450.5 6.5 convolution_add_fusion.5
  1457.0 8.8 convolution_add_fusion.4
  1468.3 132.7 %collective-permute-done.1 = bf16[4016,512]{1,0:T(8,128)(2,1)} collective-permute-done((bf16[4016,512]{1,0:T(8,128)(2,1)}, bf16[4016,512]{1,0:T(8,128)(2,1)}, u32[]{:S(2)}, u32[]{:S(2)}) %collective-permute-start.1) | collective-permute-done | bytes 4112416 | tf_op jit(solution)/shard_map/while/body/eval_jaxpr/ppermute | solution.py:53
  1605.4 9.2 multiply_convert_fusion.5
  1614.6 6.5 convolution_add_fusion.5
  1621.1 8.8 convolution_add_fusion.4
  1633.1 113.9 %psum.7 = f32[1]{0:T(128)} all-reduce(f32[1]{0:T(128)} %bitcast), channel_id=1, replica_groups=mesh['dp'=2,'fsdp'=8] {'fsdp'}, use_global_device_ids=true, to_apply=%region_9.10 | all-reduce | flops 1 | bytes 8 | tf_op jit(solution)/shard_map/psum | solution.py:42
  1747.0 7.6 copy.36
  (110 shorter events, 154.2 us)
Async XLA Ops:
  0.6 9.0 copy-start.3
  5.1 4.6 copy-start.1
  9.7 8.0 copy-start.2
  25.7 47.3 %collective-permute-start = (bf16[4016,512]{1,0:T(8,128)(2,1)}, bf16[4016,512]{1,0:T(8,128)(2,1)}, u32[]{:S(2)}, u32[]{:S(2)}) collective-permute-start(bf16[4016,512]{1,0:T(8,128)(2,1)} %get-tuple-element.651), channel_id=1, source_target_pairs={{0,1},{1,2},{2,3},{3,4},{4,5},{5,6},{6,7},{7,0},{8,9},{9,10},{10,1... | collective-permute-start | bytes 12337160 | tf_op jit(solution)/shard_map/while/body/eval_jaxpr/ppermute | solution.py:35
  88.1 47.1 %collective-permute-start = (bf16[4016,512]{1,0:T(8,128)(2,1)}, bf16[4016,512]{1,0:T(8,128)(2,1)}, u32[]{:S(2)}, u32[]{:S(2)}) collective-permute-start(bf16[4016,512]{1,0:T(8,128)(2,1)} %get-tuple-element.651), channel_id=1, source_target_pairs={{0,1},{1,2},{2,3},{3,4},{4,5},{5,6},{6,7},{7,0},{8,9},{9,10},{10,1... | collective-permute-start | bytes 12337160 | tf_op jit(solution)/shard_map/while/body/eval_jaxpr/ppermute | solution.py:35
  150.4 47.1 %collective-permute-start = (bf16[4016,512]{1,0:T(8,128)(2,1)}, bf16[4016,512]{1,0:T(8,128)(2,1)}, u32[]{:S(2)}, u32[]{:S(2)}) collective-permute-start(bf16[4016,512]{1,0:T(8,128)(2,1)} %get-tuple-element.651), channel_id=1, source_target_pairs={{0,1},{1,2},{2,3},{3,4},{4,5},{5,6},{6,7},{7,0},{8,9},{9,10},{10,1... | collective-permute-start | bytes 12337160 | tf_op jit(solution)/shard_map/while/body/eval_jaxpr/ppermute | solution.py:35
  212.6 47.1 %collective-permute-start = (bf16[4016,512]{1,0:T(8,128)(2,1)}, bf16[4016,512]{1,0:T(8,128)(2,1)}, u32[]{:S(2)}, u32[]{:S(2)}) collective-permute-start(bf16[4016,512]{1,0:T(8,128)(2,1)} %get-tuple-element.651), channel_id=1, source_target_pairs={{0,1},{1,2},{2,3},{3,4},{4,5},{5,6},{6,7},{7,0},{8,9},{9,10},{10,1... | collective-permute-start | bytes 12337160 | tf_op jit(solution)/shard_map/while/body/eval_jaxpr/ppermute | solution.py:35
  274.9 47.1 %collective-permute-start = (bf16[4016,512]{1,0:T(8,128)(2,1)}, bf16[4016,512]{1,0:T(8,128)(2,1)}, u32[]{:S(2)}, u32[]{:S(2)}) collective-permute-start(bf16[4016,512]{1,0:T(8,128)(2,1)} %get-tuple-element.651), channel_id=1, source_target_pairs={{0,1},{1,2},{2,3},{3,4},{4,5},{5,6},{6,7},{7,0},{8,9},{9,10},{10,1... | collective-permute-start | bytes 12337160 | tf_op jit(solution)/shard_map/while/body/eval_jaxpr/ppermute | solution.py:35
  337.1 47.1 %collective-permute-start = (bf16[4016,512]{1,0:T(8,128)(2,1)}, bf16[4016,512]{1,0:T(8,128)(2,1)}, u32[]{:S(2)}, u32[]{:S(2)}) collective-permute-start(bf16[4016,512]{1,0:T(8,128)(2,1)} %get-tuple-element.651), channel_id=1, source_target_pairs={{0,1},{1,2},{2,3},{3,4},{4,5},{5,6},{6,7},{7,0},{8,9},{9,10},{10,1... | collective-permute-start | bytes 12337160 | tf_op jit(solution)/shard_map/while/body/eval_jaxpr/ppermute | solution.py:35
  399.3 47.1 %collective-permute-start = (bf16[4016,512]{1,0:T(8,128)(2,1)}, bf16[4016,512]{1,0:T(8,128)(2,1)}, u32[]{:S(2)}, u32[]{:S(2)}) collective-permute-start(bf16[4016,512]{1,0:T(8,128)(2,1)} %get-tuple-element.651), channel_id=1, source_target_pairs={{0,1},{1,2},{2,3},{3,4},{4,5},{5,6},{6,7},{7,0},{8,9},{9,10},{10,1... | collective-permute-start | bytes 12337160 | tf_op jit(solution)/shard_map/while/body/eval_jaxpr/ppermute | solution.py:35
  462.2 11.5 copy-start
  481.2 155.3 %collective-permute-start.2 = (f32[4016,512]{1,0:T(8,128)}, f32[4016,512]{1,0:T(8,128)}, u32[]{:S(2)}, u32[]{:S(2)}) collective-permute-start(f32[4016,512]{1,0:T(8,128)} %get-tuple-element.691), channel_id=1, source_target_pairs={{0,1},{1,2},{2,3},{3,4},{4,5},{5,6},{6,7},{7,0},{8,9},{9,10},{10,1... | collective-permute-start | bytes 24674312 | tf_op jit(solution)/shard_map/while/body/eval_jaxpr/ppermute | solution.py:54
  483.7 132.7 %collective-permute-start.1 = (bf16[4016,512]{1,0:T(8,128)(2,1)}, bf16[4016,512]{1,0:T(8,128)(2,1)}, u32[]{:S(2)}, u32[]{:S(2)}) collective-permute-start(bf16[4016,512]{1,0:T(8,128)(2,1)} %get-tuple-element.690), channel_id=1, source_target_pairs={{0,1},{1,2},{2,3},{3,4},{4,5},{5,6},{6,7},{7,0},{8,9},{9,10},{10,1... | collective-permute-start | bytes 12337160 | tf_op jit(solution)/shard_map/while/body/eval_jaxpr/ppermute | solution.py:53
  645.3 155.3 %collective-permute-start.2 = (f32[4016,512]{1,0:T(8,128)}, f32[4016,512]{1,0:T(8,128)}, u32[]{:S(2)}, u32[]{:S(2)}) collective-permute-start(f32[4016,512]{1,0:T(8,128)} %get-tuple-element.691), channel_id=1, source_target_pairs={{0,1},{1,2},{2,3},{3,4},{4,5},{5,6},{6,7},{7,0},{8,9},{9,10},{10,1... | collective-permute-start | bytes 24674312 | tf_op jit(solution)/shard_map/while/body/eval_jaxpr/ppermute | solution.py:54
  647.8 132.7 %collective-permute-start.1 = (bf16[4016,512]{1,0:T(8,128)(2,1)}, bf16[4016,512]{1,0:T(8,128)(2,1)}, u32[]{:S(2)}, u32[]{:S(2)}) collective-permute-start(bf16[4016,512]{1,0:T(8,128)(2,1)} %get-tuple-element.690), channel_id=1, source_target_pairs={{0,1},{1,2},{2,3},{3,4},{4,5},{5,6},{6,7},{7,0},{8,9},{9,10},{10,1... | collective-permute-start | bytes 12337160 | tf_op jit(solution)/shard_map/while/body/eval_jaxpr/ppermute | solution.py:53
  809.4 155.3 %collective-permute-start.2 = (f32[4016,512]{1,0:T(8,128)}, f32[4016,512]{1,0:T(8,128)}, u32[]{:S(2)}, u32[]{:S(2)}) collective-permute-start(f32[4016,512]{1,0:T(8,128)} %get-tuple-element.691), channel_id=1, source_target_pairs={{0,1},{1,2},{2,3},{3,4},{4,5},{5,6},{6,7},{7,0},{8,9},{9,10},{10,1... | collective-permute-start | bytes 24674312 | tf_op jit(solution)/shard_map/while/body/eval_jaxpr/ppermute | solution.py:54
  811.9 132.7 %collective-permute-start.1 = (bf16[4016,512]{1,0:T(8,128)(2,1)}, bf16[4016,512]{1,0:T(8,128)(2,1)}, u32[]{:S(2)}, u32[]{:S(2)}) collective-permute-start(bf16[4016,512]{1,0:T(8,128)(2,1)} %get-tuple-element.690), channel_id=1, source_target_pairs={{0,1},{1,2},{2,3},{3,4},{4,5},{5,6},{6,7},{7,0},{8,9},{9,10},{10,1... | collective-permute-start | bytes 12337160 | tf_op jit(solution)/shard_map/while/body/eval_jaxpr/ppermute | solution.py:53
  973.5 155.3 %collective-permute-start.2 = (f32[4016,512]{1,0:T(8,128)}, f32[4016,512]{1,0:T(8,128)}, u32[]{:S(2)}, u32[]{:S(2)}) collective-permute-start(f32[4016,512]{1,0:T(8,128)} %get-tuple-element.691), channel_id=1, source_target_pairs={{0,1},{1,2},{2,3},{3,4},{4,5},{5,6},{6,7},{7,0},{8,9},{9,10},{10,1... | collective-permute-start | bytes 24674312 | tf_op jit(solution)/shard_map/while/body/eval_jaxpr/ppermute | solution.py:54
  976.0 132.7 %collective-permute-start.1 = (bf16[4016,512]{1,0:T(8,128)(2,1)}, bf16[4016,512]{1,0:T(8,128)(2,1)}, u32[]{:S(2)}, u32[]{:S(2)}) collective-permute-start(bf16[4016,512]{1,0:T(8,128)(2,1)} %get-tuple-element.690), channel_id=1, source_target_pairs={{0,1},{1,2},{2,3},{3,4},{4,5},{5,6},{6,7},{7,0},{8,9},{9,10},{10,1... | collective-permute-start | bytes 12337160 | tf_op jit(solution)/shard_map/while/body/eval_jaxpr/ppermute | solution.py:53
  1137.6 155.3 %collective-permute-start.2 = (f32[4016,512]{1,0:T(8,128)}, f32[4016,512]{1,0:T(8,128)}, u32[]{:S(2)}, u32[]{:S(2)}) collective-permute-start(f32[4016,512]{1,0:T(8,128)} %get-tuple-element.691), channel_id=1, source_target_pairs={{0,1},{1,2},{2,3},{3,4},{4,5},{5,6},{6,7},{7,0},{8,9},{9,10},{10,1... | collective-permute-start | bytes 24674312 | tf_op jit(solution)/shard_map/while/body/eval_jaxpr/ppermute | solution.py:54
  1140.1 132.7 %collective-permute-start.1 = (bf16[4016,512]{1,0:T(8,128)(2,1)}, bf16[4016,512]{1,0:T(8,128)(2,1)}, u32[]{:S(2)}, u32[]{:S(2)}) collective-permute-start(bf16[4016,512]{1,0:T(8,128)(2,1)} %get-tuple-element.690), channel_id=1, source_target_pairs={{0,1},{1,2},{2,3},{3,4},{4,5},{5,6},{6,7},{7,0},{8,9},{9,10},{10,1... | collective-permute-start | bytes 12337160 | tf_op jit(solution)/shard_map/while/body/eval_jaxpr/ppermute | solution.py:53
  1301.7 155.3 %collective-permute-start.2 = (f32[4016,512]{1,0:T(8,128)}, f32[4016,512]{1,0:T(8,128)}, u32[]{:S(2)}, u32[]{:S(2)}) collective-permute-start(f32[4016,512]{1,0:T(8,128)} %get-tuple-element.691), channel_id=1, source_target_pairs={{0,1},{1,2},{2,3},{3,4},{4,5},{5,6},{6,7},{7,0},{8,9},{9,10},{10,1... | collective-permute-start | bytes 24674312 | tf_op jit(solution)/shard_map/while/body/eval_jaxpr/ppermute | solution.py:54
  1304.2 132.7 %collective-permute-start.1 = (bf16[4016,512]{1,0:T(8,128)(2,1)}, bf16[4016,512]{1,0:T(8,128)(2,1)}, u32[]{:S(2)}, u32[]{:S(2)}) collective-permute-start(bf16[4016,512]{1,0:T(8,128)(2,1)} %get-tuple-element.690), channel_id=1, source_target_pairs={{0,1},{1,2},{2,3},{3,4},{4,5},{5,6},{6,7},{7,0},{8,9},{9,10},{10,1... | collective-permute-start | bytes 12337160 | tf_op jit(solution)/shard_map/while/body/eval_jaxpr/ppermute | solution.py:53
  1465.8 155.3 %collective-permute-start.2 = (f32[4016,512]{1,0:T(8,128)}, f32[4016,512]{1,0:T(8,128)}, u32[]{:S(2)}, u32[]{:S(2)}) collective-permute-start(f32[4016,512]{1,0:T(8,128)} %get-tuple-element.691), channel_id=1, source_target_pairs={{0,1},{1,2},{2,3},{3,4},{4,5},{5,6},{6,7},{7,0},{8,9},{9,10},{10,1... | collective-permute-start | bytes 24674312 | tf_op jit(solution)/shard_map/while/body/eval_jaxpr/ppermute | solution.py:54
  1468.3 132.7 %collective-permute-start.1 = (bf16[4016,512]{1,0:T(8,128)(2,1)}, bf16[4016,512]{1,0:T(8,128)(2,1)}, u32[]{:S(2)}, u32[]{:S(2)}) collective-permute-start(bf16[4016,512]{1,0:T(8,128)(2,1)} %get-tuple-element.690), channel_id=1, source_target_pairs={{0,1},{1,2},{2,3},{3,4},{4,5},{5,6},{6,7},{7,0},{8,9},{9,10},{10,1... | collective-permute-start | bytes 12337160 | tf_op jit(solution)/shard_map/while/body/eval_jaxpr/ppermute | solution.py:53
  1629.9 124.7 %copy-start.4 = (f32[1024,512]{1,0:T(8,128)}, f32[1024,512]{1,0:T(8,128)S(1)}, u32[]{:S(2)}) copy-start(f32[1024,512]{1,0:T(8,128)S(1)} %get-tuple-element.719) | copy-start | bytes 6291460
  1629.9 117.1 %collective-permute-start.3 = (f32[4016,512]{1,0:T(8,128)}, f32[4016,512]{1,0:T(8,128)}, u32[]{:S(2)}, u32[]{:S(2)}) collective-permute-start(f32[4016,512]{1,0:T(8,128)} %get-tuple-element.452), channel_id=1, source_target_pairs={{0,1},{1,2},{2,3},{3,4},{4,5},{5,6},{6,7},{7,0},{8,9},{9,10},{10,1... | collective-permute-start | bytes 24674312 | tf_op jit(solution)/shard_map/ppermute | solution.py:60
where the time goes:
time: 1760 us; the launch traced here: 1750 us
  waiting for transfers between devices  1240 us (70%)
  matrix products  241 us (14%)
  blocking collectives  114 us (6%)
  local copies, waits for them, and re-layouts  80.1 us (5%)
  other arithmetic  39.2 us (2%)
  starting transfers between devices  37.9 us (2%)
    ppermute x7, waiting for transfers between devices, bwd_body(): w_cur = lax.ppermute(w_cur, 'fsdp', ring_pairs)  929 us
    ppermute x7, waiting for transfers between devices, fwd_body(): w_cur = lax.ppermute(w_cur, 'fsdp', ring_pairs)  312 us
    dot_general x15, matrix products, block_logits(): lax.dot_general(hidden, w_blk, (((1,), (1,)), ((), ())), preferred_elemen...  117 us
    psum x1, blocking collectives, local_head(): lax.psum(jnp.sum(log_norm - tgt_logit) / tokens, 'fsdp').reshape(1)  114 us
    dot_general x8, matrix products, bwd_update(): lax.dot_general(dlogits, hidden, (((0,), (0,)), ((), ())), preferred_elem...  69 us
    while x21, local copies, waits for them, and re-layouts  61.4 us
    dot_general x8, matrix products, bwd_update(): dh_part = jnp.dot(dlogits, w_blk, preferred_element_type=jnp.float32)  55.2 us
    reduce_sum x8, other arithmetic, fwd_update(): tgt_logit = tgt_logit + jnp.sum(jnp.where(is_target, logits, 0.0), axis=1)  38.4 us
  transfers between devices with their start and end apart: 22, of which 14 were waited for; matrix products, arithmetic and copies ran while one was open for 8% of the time, Pallas kernels for 0%

commit v1 on v0

v1 whole, which is shorter than its diff:
```python
import functools

import jax
import jax.numpy as jnp
from jax import lax
from jax.experimental import pallas as pl
from jax.experimental.pallas import tpu as pltpu
from jax.sharding import PartitionSpec as P

F32 = jnp.float32
BF16 = jnp.bfloat16
TOK_TILE = 512
ROW_CHUNK = 1008


def row_chunks(rows):
    return [(start, min(ROW_CHUNK, rows - start)) for start in range(0, rows, ROW_CHUNK)]


def fwd_kernel(w_ref, h_ref, max_ref, sum_ref, z_ref):
    rows = w_ref.shape[0]
    toks = h_ref.shape[0]
    run_max = jnp.full((8, toks), -jnp.inf, F32)
    run_sum = jnp.zeros((8, toks), F32)
    for idx, (start, size) in enumerate(row_chunks(rows)):
        z_new = lax.dot_general(w_ref[start:start + size, :], h_ref[...], (((1,), (1,)), ((), ())), preferred_element_type=F32)
        z_ref[start:start + size, :] = z_new
        z_grp = z_ref[start:start + size, :].reshape(size // 8, 8, toks)
        new_max = jnp.maximum(run_max, jnp.max(z_grp, axis=0))
        run_sum = run_sum * jnp.exp(run_max - new_max) + jnp.sum(jnp.exp(z_grp - new_max[None]), axis=0)
        run_max = new_max
    tot_max = jnp.max(run_max, axis=0, keepdims=True)
    max_ref[...] = tot_max
    sum_ref[...] = jnp.sum(run_sum * jnp.exp(run_max - tot_max), axis=0, keepdims=True)


def bwd_kernel(inv_tokens, w_ref, h_ref, shift_ref, tgt_ref, dh_ref, dw_ref, zt_ref, z_ref, dz_ref):
    rows = w_ref.shape[0]
    toks = h_ref.shape[0]

    @pl.when(pl.program_id(0) == 0)
    def _():
        dw_ref[...] = jnp.zeros_like(dw_ref)

    shift = shift_ref[...]
    tgt = tgt_ref[...]
    zt_sum = jnp.zeros((8, toks), F32)
    for idx, (start, size) in enumerate(row_chunks(rows)):
        z_ref[start:start + size, :] = lax.dot_general(w_ref[start:start + size, :], h_ref[...], (((1,), (1,)), ((), ())), preferred_element_type=F32)
        z = z_ref[start:start + size, :]
        mask = (lax.broadcasted_iota(jnp.int32, (size, toks), 0) + start) == tgt
        prob = jnp.exp(z - shift)
        dz = jnp.where(mask, prob - inv_tokens, prob).astype(BF16)
        zt_sum += jnp.sum(jnp.where(mask, z, 0.0).reshape(size // 8, 8, toks), axis=0)
        dz_ref[start:start + size, :] = dz
        dw_ref[start:start + size, :] += jnp.dot(dz_ref[start:start + size, :], h_ref[...], preferred_element_type=F32)
        dh_part = lax.dot_general(dz_ref[start:start + size, :], w_ref[start:start + size, :], (((0,), (0,)), ((), ())), preferred_element_type=F32)
        if idx == 0:
            dh_ref[...] = dh_part
        else:
            dh_ref[...] += dh_part
    zt_ref[...] = jnp.sum(zt_sum, axis=0, keepdims=True)


def solution(mesh):
    groups = mesh.shape["fsdp"]
    tok_spec = P(("dp", "fsdp"), None)

    def local_head(hidden, targets, weight):
        tok_loc, width = hidden.shape
        rows = weight.shape[0]
        tokens = tok_loc * groups
        tiles = tokens // TOK_TILE
        rank = lax.axis_index("fsdp")
        h_all = lax.all_gather(hidden, "fsdp", tiled=True)
        t_all = (lax.all_gather(targets, "fsdp", tiled=True) - rank * rows).reshape(1, tokens)
        whole_w = pl.BlockSpec((rows, width), lambda i: (0, 0))
        h_spec = pl.BlockSpec((TOK_TILE, width), lambda i: (i, 0))
        row_spec = pl.BlockSpec((1, TOK_TILE), lambda i: (0, i))
        row_shape = jax.ShapeDtypeStruct((1, tokens), F32)
        loc_max, loc_sum = pl.pallas_call(
            fwd_kernel,
            grid=(tiles,),
            in_specs=[whole_w, h_spec],
            out_specs=[row_spec, row_spec],
            out_shape=[row_shape, row_shape],
            scratch_shapes=[pltpu.VMEM((rows, TOK_TILE), F32)],
            name="fwd_stats",
        )(weight, h_all)
        all_max = lax.pmax(loc_max, "fsdp")
        all_sum = lax.psum(loc_sum * jnp.exp(loc_max - all_max), "fsdp")
        lse = all_max + jnp.log(all_sum)
        shift = lse + jnp.log(jnp.float32(tokens))
        dh_part, grad_w, zt = pl.pallas_call(
            functools.partial(bwd_kernel, 1.0 / tokens),
            grid=(tiles,),
            in_specs=[whole_w, h_spec, row_spec, row_spec],
            out_specs=[h_spec, whole_w, row_spec],
            out_shape=[jax.ShapeDtypeStruct((tokens, width), F32), jax.ShapeDtypeStruct((rows, width), F32), row_shape],
            scratch_shapes=[pltpu.VMEM((rows, TOK_TILE), F32), pltpu.VMEM((rows, TOK_TILE), BF16)],
            name="bwd_grads",
        )(weight, h_all, shift, t_all)
        grad_h = lax.psum_scatter(dh_part, "fsdp", scatter_dimension=0, tiled=True)
        loss_val = ((jnp.sum(lse) - lax.psum(jnp.sum(zt), "fsdp")) / tokens).reshape(1)
        return loss_val, grad_h, grad_w

    return jax.shard_map(local_head, mesh=mesh, in_specs=(tok_spec, P(("dp", "fsdp")), P("fsdp", None)), out_specs=(P("dp"), tok_spec, tok_spec), check_vma=False)
```

time: 1760 us -> 391 us (0.22)
  waiting for transfers between devices: 1240 us -> 102 us
  matrix products: 241 us -> 0 us
  Pallas kernels: 0 us -> 186 us
  local copies, waits for them, and re-layouts: 80.1 us -> 0.7 us
  starting transfers between devices: 37.9 us -> 0.12 us
  other arithmetic: 39.2 us -> 3.39 us
  blocking collectives: 114 us -> 81.4 us
    ppermute x22 -> x0, waiting for transfers between devices: 1240 us -> none  [the longest x7 929 us: bwd_body(): w_cur = lax.ppermute(w_cur, 'fsdp', ring_pairs)]
    dot_general x31 -> x0, matrix products: 241 us -> none  [the longest x15 117 us: block_logits(): lax.dot_general(hidden, w_blk, (((1,), (1,)), ((), ())), preferred_elemen...]
    pallas_call x0 -> x2, Pallas kernels: none -> 186 us  [the longest x1 130 us: local_head(): pl.pallas_call(functools.partial(bwd_kernel, 1.0 / tokens), grid=(tiles,)...]
    psum x1 -> x2, blocking collectives: 114 us -> 39.9 us  [the longest x1 23.9 us: local_head(): all_sum = lax.psum(loc_sum * jnp.exp(loc_max - all_max), 'fsdp')]
    reduce_scatter x0 -> x1, waiting for transfers between devices: none -> 70.8 us  [local_head(): grad_h = lax.psum_scatter(dh_part, 'fsdp', scatter_dimension=0, tiled=True)]
    while x21 -> x0, local copies, waits for them, and re-layouts: 61.4 us -> none
    reduce_sum x9 -> x1, other arithmetic: 39 us -> 0.66 us  [local_head(): jnp.sum(zt)]
    ppermute x22 -> x0, starting transfers between devices: 37.9 us -> none  [the longest x7 17.7 us: fwd_body(): w_cur = lax.ppermute(w_cur, 'fsdp', ring_pairs)]
  transfers between devices with their start and end apart: 22 -> 2, of which waited for: 14 -> 2; matrix products, arithmetic and copies ran while one was open for 8% -> 0% of each run, Pallas kernels for 0% -> 0%
where the time goes in v1:
time: 391 us; the launch traced here: 390 us
  Pallas kernels  186 us (48%)
  waiting for transfers between devices  102 us (26%)
  blocking collectives  81.4 us (21%)
  between operations  16.4 us (4%)
    pallas_call x1, Pallas kernels, local_head(): pl.pallas_call(functools.partial(bwd_kernel, 1.0 / tokens), grid=(tiles,)...  130 us
    reduce_scatter x1, waiting for transfers between devices, local_head(): grad_h = lax.psum_scatter(dh_part, 'fsdp', scatter_dimension=0, tiled=True)  70.8 us
    pallas_call x1, Pallas kernels, local_head(): pl.pallas_call(fwd_kernel, grid=(tiles,), in_specs=[whole_w, h_spec], out...  56.6 us
    all_gather x1, waiting for transfers between devices, local_head(): h_all = lax.all_gather(hidden, 'fsdp', tiled=True)  30.1 us
    psum x1, blocking collectives, local_head(): all_sum = lax.psum(loc_sum * jnp.exp(loc_max - all_max), 'fsdp')  23.9 us
    pmax x1, blocking collectives, local_head(): all_max = lax.pmax(loc_max, 'fsdp')  21.6 us
    all_gather x1, blocking collectives, local_head(): lax.all_gather(targets, 'fsdp', tiled=True) - rank * rows  19.9 us
    psum x1, blocking collectives, local_head(): lax.psum(jnp.sum(zt), 'fsdp')  16.1 us
  transfers between devices with their start and end apart: 2, of which 2 were waited for; matrix products, arithmetic and copies ran while one was open for 0% of the time, Pallas kernels for 0%

profile of v1, /device:TPU:113, one launch (start us, length us, event | category | flops | bytes accessed | tf_op | source)
XLA Modules:
  0.0 390.2 jit_solution(8812279478024556126)
XLA Ops:
  7.2 0.1 all-gather.2.cloned.1.call-start
  7.2 0.7 all-gather.2.cloned.1.call-update
  8.0 0.1 reduce-scatter.2.cloned.1.call-start
  8.0 19.9 %all_gather.7 = s32[8192]{0:T(1024)S(1)} all-gather(s32[1024]{0:T(1024)} %param.4), channel_id=1, replica_groups=mesh['dp'=2,'fsdp'=8] {'fsdp'}, dimensions={0}, use_global_device_ids=true | all-gather | bytes 36864 | tf_op jit(solution)/shard_map/all_gather | solution.py:76
  28.0 0.6 broadcast_subtract_fusion
  28.6 30.1 %all-gather.2.cloned.1.call-done.h_ref = bf16[8192,512]{1,0:T(8,128)(2,1)} async-done(((bf16[1024,512]{1,0:T(8,128)(2,1)}), bf16[8192,512]{1,0:T(8,128)(2,1)}) %all-gather.2.cloned.1.call-update) | async-done | bytes 8388624 | tf_op jit(solution)/shard_map/all_gather | solution.py:75
  58.7 56.6 %fwd_stats.1 = (f32[1,8192]{1,0:T(1,128)}, f32[1,8192]{1,0:T(1,128)}) custom-call(bf16[4016,512]{1,0:T(8,128)(2,1)} %w_ref.3, bf16[8192,512]{1,0:T(8,128)(2,1)} %all-gather.2.cloned.1.call-done.h_ref), custom_call_target="tpu_custom_call" | custom-call | tf_op jit(solution)/shard_map/fwd_stats/pallas_call | solution.py:81
  115.3 21.6 %pmax.7 = f32[1,8192]{1,0:T(1,128)S(1)} all-reduce(f32[1,8192]{1,0:T(1,128)} %get-tuple-element.8), channel_id=1, replica_groups=mesh['dp'=2,'fsdp'=8] {'fsdp'}, use_global_device_ids=true, to_apply=%region_0.0 | all-reduce | flops 8192 | bytes 65536 | tf_op jit(solution)/shard_map/pmax | solution.py:90
  136.9 0.8 exponential_multiply_fusion
  137.7 23.9 %psum.14 = f32[1,8192]{1,0:T(1,128)S(1)} all-reduce(f32[1,8192]{1,0:T(1,128)S(1)} %exponential_multiply_fusion), channel_id=1, replica_groups=mesh['dp'=2,'fsdp'=8] {'fsdp'}, use_global_device_ids=true, to_apply=%region_1.0 | all-reduce | flops 8192 | bytes 65536 | tf_op jit(solution)/shard_map/psum | solution.py:91
  161.6 1.3 broadcast_add_fusion
  162.9 129.9 %bwd_grads.1 = (f32[8192,512]{1,0:T(8,128)}, f32[4016,512]{1,0:T(8,128)}, f32[1,8192]{1,0:T(1,128)}) custom-call(bf16[4016,512]{1,0:T(8,128)(2,1)} %w_ref.3, bf16[8192,512]{1,0:T(8,128)(2,1)} %all-gather.2.cloned.1.call-done.h_ref, f32[1,8192]{1,0:T(1,128)} %get-tuple-element.13.shift_ref, s32[1,8192]{1,0:T(1,128)} %bitcast.2), custom_call_target="tpu_custom_call" | custom-call | tf_op jit(solution)/shard_map/bwd_grads/pallas_call | solution.py:94
  292.7 0.0 copy-start
  292.7 0.1 reduce-scatter.2.cloned.1.call-update
  292.8 0.7 copy-done
  293.5 0.7 reduce_sum.19
  294.1 16.1 %psum.15 = f32[]{:T(128)} all-reduce(f32[]{:T(128)} %reduce_sum.19), channel_id=1, replica_groups=mesh['dp'=2,'fsdp'=8] {'fsdp'}, use_global_device_ids=true, to_apply=%region_4.0 | all-reduce | flops 1 | bytes 8 | tf_op jit(solution)/shard_map/psum | solution.py:104
  311.4 70.8 %reduce-scatter.2.cloned.1.call-done = f32[1024,512]{1,0:T(8,128)} async-done(((f32[8192,512]{1,0:T(8,128)}), f32[1024,512]{1,0:T(8,128)}) %reduce-scatter.2.cloned.1.call-update) | async-done | bytes 2097168 | tf_op jit(solution)/shard_map/reduce_scatter | solution.py:103
Async XLA Ops:
  7.2 51.5 %all-gather.2.cloned.1.call-start = ((), (), s32[]{:S(2)}) async-start(), calls=%async_computation.1 | async-start | bytes 9437184 | tf_op jit(solution)/shard_map/all_gather | solution.py:75
  8.0 374.3 %reduce-scatter.2.cloned.1.call-start = ((), (), s32[]{:S(2)}) async-start(), calls=%async_computation.2 | async-start | bytes 18874368 | tf_op jit(solution)/shard_map/reduce_scatter | solution.py:103
  292.7 0.8 copy-start
Sparse Core Ops, SparseCore 0:
  9.6 49.0 all-gather.1
  292.9 89.3 reduce-scatter.1

commit v2 on v0

v2 whole, which is shorter than its diff:
```python
import functools

import jax
import jax.numpy as jnp
from jax import lax
from jax.experimental import pallas as pl
from jax.experimental.pallas import tpu as pltpu
from jax.sharding import PartitionSpec as P

F32 = jnp.float32
BF16 = jnp.bfloat16
MESH = pl.DeviceIdType.MESH
CORES = 2
ROW_CHUNK = 1008

LEFT, RIGHT, ACROSS = 3, 1, 2
PEERS = [(0, 1), (LEFT, 0), (LEFT, 1), (RIGHT, 0), (RIGHT, 1), (ACROSS, 0), (ACROSS, 1)]
PEER_SLOT = {peer: slot for slot, peer in enumerate(PEERS)}

PAIR_DX = [ACROSS, ACROSS, RIGHT, LEFT, RIGHT, LEFT, 0, 0]
PAIR_HALF = [0, 1, 1, 0, 0, 1, 0, 1]
DX_CODE = sum(v << (2 * q) for q, v in enumerate(PAIR_DX))
HALF_CODE = sum(v << (2 * q) for q, v in enumerate(PAIR_HALF))


def row_chunks(rows):
    return [(start, min(ROW_CHUNK, rows - start)) for start in range(0, rows, ROW_CHUNK)]


def head_kernel(groups, tokens, hid_hbm, tgt_hbm, w_hbm, loss_ref, dh_hbm, dw_hbm,
                h_all, t_all, w_ref, z_ref, dz_ref, dw_ref, pbuf, d2d_in, ring_in, fin_in,
                stat_loc, stat_in, lse_acc, zt_acc, zt_row, zt_in,
                load_sem, ag_send, ag_recv, tgt_send, tgt_recv, stat_send, stat_recv,
                d2d_send, d2d_recv, ici_send, ring_recv, fin_recv, zt_send, zt_recv, out_sem):
    chips = groups // CORES
    me = lax.axis_index("fsdp")
    chip = lax.div(me, CORES)
    core = lax.rem(me, CORES)
    rows, width = w_ref.shape
    half_toks = h_all.shape[2]

    def dev(dx, flip):
        return lax.rem(chip + dx, chips) * CORES + lax.rem(core + flip, CORES)

    def seen_from(peer):
        return PEER_SLOT[((chips - peer[0]) % chips, peer[1])]

    load_h = pltpu.make_async_copy(hid_hbm, h_all.at[me], load_sem.at[0])
    load_t = pltpu.make_async_copy(tgt_hbm, t_all.at[me], load_sem.at[1])
    load_w = pltpu.make_async_copy(w_hbm, w_ref, load_sem.at[2])
    load_h.start()
    load_t.start()
    load_w.start()
    barrier = pltpu.get_barrier_semaphore()
    for peer in PEERS:
        pl.semaphore_signal(barrier, inc=1, device_id={"fsdp": dev(*peer)}, device_id_type=MESH)
    dw_ref[...] = jnp.zeros_like(dw_ref)
    lse_acc[...] = jnp.zeros_like(lse_acc)
    zt_acc[...] = jnp.zeros_like(zt_acc)
    load_h.wait()
    load_t.wait()
    pl.semaphore_wait(barrier, len(PEERS))

    def gather_copy(owner, half, to):
        block = dev(*owner)
        as_seen = PEER_SLOT[((owner[0] - to[0]) % chips, (owner[1] + to[1]) % CORES)]
        idx = as_seen * 2 + half
        return pltpu.make_async_remote_copy(
            src_ref=h_all.at[block, half], dst_ref=h_all.at[block, half], send_sem=ag_send.at[idx], recv_sem=ag_recv.at[idx],
            device_id={"fsdp": dev(*to)}, device_id_type=MESH)

    def gather_recv(owner, half):
        block = dev(*owner)
        idx = PEER_SLOT[owner] * 2 + half
        pltpu.make_async_remote_copy(
            src_ref=h_all.at[block, half], dst_ref=h_all.at[block, half], send_sem=ag_send.at[idx], recv_sem=ag_recv.at[idx],
            device_id={"fsdp": me}, device_id_type=MESH).wait_recv()

    own, partner, left, right, across = (0, 0), (0, 1), (LEFT, 0), (RIGHT, 0), (ACROSS, 0)
    for half, to in [(0, right), (1, left), (0, partner), (1, partner), (1, right), (0, left)]:
        gather_copy(own, half, to).start()

    def target_copy(peer):
        slot = seen_from(peer)
        return pltpu.make_async_remote_copy(
            src_ref=t_all.at[me], dst_ref=t_all.at[me], send_sem=tgt_send.at[slot], recv_sem=tgt_recv.at[slot],
            device_id={"fsdp": dev(*peer)}, device_id_type=MESH)

    for peer in PEERS:
        target_copy(peer).start()
    load_w.wait()

    def stat_copy(peer, block, half):
        return pltpu.make_async_remote_copy(
            src_ref=stat_loc.at[block, half], dst_ref=stat_in.at[seen_from(peer), block, half],
            send_sem=stat_send, recv_sem=stat_recv, device_id={"fsdp": dev(*peer)}, device_id_type=MESH)

    def fwd_step(step, carry):
        grp = lax.div(step, 4)
        sub = lax.rem(step, 4)
        flip = lax.div(sub, 2)
        side = lax.rem(sub, 2)
        dx = lax.rem(lax.div(grp + 1, 2), 2) * (LEFT + (RIGHT - LEFT) * side) + lax.div(grp, 3) * ACROSS
        half = side + lax.div(grp, 2) * (1 - lax.div(grp, 3)) * (1 - 2 * side)
        block = dev(dx, flip)

        @pl.when(step == 2)
        def _():
            gather_recv(partner, 0)
            gather_recv(partner, 1)

        @pl.when(step == 4)
        def _():
            gather_recv(left, 0)
            gather_copy(left, 0, right).start()
            gather_copy(left, 0, partner).start()
            gather_recv(right, 1)
            gather_copy(right, 1, left).start()
            gather_copy(right, 1, partner).start()

        @pl.when(step == 6)
        def _():
            gather_recv((LEFT, 1), 0)
            gather_recv((RIGHT, 1), 1)

        @pl.when(step == 8)
        def _():
            gather_recv(left, 1)
            gather_copy(left, 1, partner).start()
            gather_recv(right, 0)
            gather_copy(right, 0, partner).start()

        @pl.when(step == 10)
        def _():
            gather_recv((LEFT, 1), 1)
            gather_recv((RIGHT, 1), 0)

        @pl.when(step == 12)
        def _():
            gather_recv(across, 0)
            gather_copy(across, 0, partner).start()
            gather_recv(across, 1)
            gather_copy(across, 1, partner).start()

        @pl.when(step == 14)
        def _():
            gather_recv((ACROSS, 1), 0)
            gather_recv((ACROSS, 1), 1)

        run_max = jnp.full((8, half_toks), -jnp.inf, F32)
        run_sum = jnp.zeros((8, half_toks), F32)
        for start, size in row_chunks(rows):
            z_ref[start:start + size, :] = lax.dot_general(
                w_ref[start:start + size, :], h_all[block, half], (((1,), (1,)), ((), ())), preferred_element_type=F32)
            z_grp = z_ref[start:start + size, :].reshape(size // 8, 8, half_toks)
            new_max = jnp.maximum(run_max, jnp.max(z_grp, axis=0))
            run_sum = run_sum * jnp.exp(run_max - new_max) + jnp.sum(jnp.exp(z_grp - new_max[None]), axis=0)
            run_max = new_max
        tot_max = jnp.max(run_max, axis=0, keepdims=True)
        stat_loc[block, half, 0] = tot_max
        stat_loc[block, half, 1] = jnp.sum(run_sum * jnp.exp(run_max - tot_max), axis=0, keepdims=True)
        for peer in PEERS:
            stat_copy(peer, block, half).start()
        return carry

    lax.fori_loop(0, 2 * groups, fwd_step, 0)

    for peer in PEERS:
        target_copy(peer).wait_recv()
    all_stats = pltpu.make_async_remote_copy(
        src_ref=stat_in, dst_ref=stat_in, send_sem=stat_send, recv_sem=stat_recv, device_id={"fsdp": me}, device_id_type=MESH)
    all_stats.wait_recv()

    def d2d_copy(pair, slot):
        return pltpu.make_async_remote_copy(
            src_ref=pbuf.at[slot], dst_ref=d2d_in.at[pair], send_sem=d2d_send.at[slot], recv_sem=d2d_recv.at[pair],
            device_id={"fsdp": dev(*partner)}, device_id_type=MESH)

    def ici_copy(pair):
        dx, half = PAIR_DX[pair], PAIR_HALF[pair]
        if dx == ACROSS:
            to = right if half == 0 else left
            dst, recv = ring_in.at[half], ring_recv.at[half]
        else:
            to = (dx, 0)
            from_side = 0 if dx == RIGHT else 1
            dst, recv = fin_in.at[from_side, half], fin_recv.at[from_side * 2 + half]
        return pltpu.make_async_remote_copy(
            src_ref=pbuf.at[2 + pair], dst_ref=dst, send_sem=ici_send.at[pair], recv_sem=recv,
            device_id={"fsdp": dev(*to)}, device_id_type=MESH)

    def add_into(slot, sources):
        def body(i, carry):
            sl = pl.ds(pl.multiple_of(i * 64, 64), 64)
            tot = pbuf[slot, sl, :]
            for src in sources:
                tot = tot + src[sl, :]
            pbuf[slot, sl, :] = tot
            return carry
        lax.fori_loop(0, half_toks // 64, body, 0)

    inv_tokens = 1.0 / tokens
    log_tokens = jnp.log(jnp.float32(tokens))

    def bwd_step(step, carry):
        pair = lax.div(step, 2)
        flip = 1 - lax.rem(step, 2)
        dx = lax.rem(lax.shift_right_logical(jnp.int32(DX_CODE), 2 * pair), 4)
        half = lax.rem(lax.shift_right_logical(jnp.int32(HALF_CODE), 2 * pair), 4)
        block = dev(dx, flip)
        slot = flip * lax.rem(pair, 2) + (1 - flip) * (2 + pair)

        for pair_s in range(2, 8):
            @pl.when(step == 2 * pair_s)
            def _():
                d2d_copy(pair_s - 2, pair_s % 2).wait_send()

        maxes = [stat_loc[block, half, 0]] + [stat_in[i, block, half, 0] for i in range(len(PEERS))]
        sums = [stat_loc[block, half, 1]] + [stat_in[i, block, half, 1] for i in range(len(PEERS))]
        tot_max = functools.reduce(jnp.maximum, maxes)
        tot_sum = sum(s * jnp.exp(m - tot_max) for m, s in zip(maxes, sums))
        lse = tot_max + jnp.log(tot_sum)
        lse_acc[...] += lse
        shift = lse + log_tokens
        tgt = t_all[block, half] - me * rows
        zt_sum = zt_acc[...]
        h_tile = h_all.at[block, half]
        for idx, (start, size) in enumerate(row_chunks(rows)):
            sl = slice(start, start + size)
            z_ref[sl, :] = lax.dot_general(w_ref[sl, :], h_tile[...], (((1,), (1,)), ((), ())), preferred_element_type=F32)
            z = z_ref[sl, :]
            mask = (lax.broadcasted_iota(jnp.int32, (size, half_toks), 0) + start) == tgt
            prob = jnp.exp(z - shift)
            dz_ref[sl, :] = jnp.where(mask, prob - inv_tokens, prob).astype(BF16)
            zt_sum += jnp.sum(jnp.where(mask, z, 0.0).reshape(size // 8, 8, half_toks), axis=0)
            dw_ref[sl, :] += jnp.dot(dz_ref[sl, :], h_tile[...], preferred_element_type=F32)
            dh_part = lax.dot_general(dz_ref[sl, :], w_ref[sl, :], (((0,), (0,)), ((), ())), preferred_element_type=F32)
            if idx == 0:
                pbuf[slot] = dh_part
            else:
                pbuf[slot] += dh_part
        zt_acc[...] = zt_sum

        for pair_s in range(8):
            @pl.when(step == 2 * pair_s)
            def _():
                d2d_copy(pair_s, pair_s % 2).start()

            @pl.when(step == 2 * pair_s + 1)
            def _():
                d2d_copy(pair_s, pair_s % 2).wait_recv()
                sources = [d2d_in.at[pair_s]]
                dx_s, half_s = PAIR_DX[pair_s], PAIR_HALF[pair_s]
                if (dx_s, half_s) == (RIGHT, 0):
                    ici_copy(0).wait_recv()
                    sources.append(ring_in.at[0])
                if (dx_s, half_s) == (LEFT, 1):
                    ici_copy(1).wait_recv()
                    sources.append(ring_in.at[1])
                if dx_s == 0:
                    for pair_r in range(2, 6):
                        if PAIR_HALF[pair_r] == half_s:
                            ici_copy(pair_r).wait_recv()
                            sources.append(fin_in.at[0 if PAIR_DX[pair_r] == RIGHT else 1, half_s])
                add_into(2 + pair_s, sources)
                if dx_s == 0:
                    pltpu.make_async_copy(pbuf.at[2 + pair_s], dh_hbm.at[half_s], out_sem.at[half_s]).start()
                else:
                    ici_copy(pair_s).start()
        return carry

    lax.fori_loop(0, 2 * groups, bwd_step, 0)

    out_w = pltpu.make_async_copy(dw_ref, dw_hbm, out_sem.at[2])
    out_w.start()
    zt_row[...] = jnp.sum(zt_acc[...], axis=0, keepdims=True)

    def zt_copy(peer):
        slot = seen_from(peer)
        return pltpu.make_async_remote_copy(
            src_ref=zt_row, dst_ref=zt_in.at[slot], send_sem=zt_send.at[slot], recv_sem=zt_recv.at[slot],
            device_id={"fsdp": dev(*peer)}, device_id_type=MESH)

    for peer in PEERS:
        zt_copy(peer).start()
    for peer in PEERS:
        zt_copy(peer).wait()
    tot = lse_acc[...] - zt_row[...]
    for i in range(len(PEERS)):
        tot = tot - zt_in[i]
    loss_ref[...] = jnp.broadcast_to(jnp.sum(tot, axis=1, keepdims=True) * inv_tokens, loss_ref.shape)

    for owner, half, to in (
            [(own, h, to) for h in range(2) for to in (right, left, partner)]
            + [(left, 0, right), (right, 1, left)]
            + [(side, h, partner) for side in (left, right, across) for h in range(2)]):
        gather_copy(owner, half, to).wait_send()
    for peer in PEERS:
        target_copy(peer).wait_send()
    all_stats.wait_send()
    d2d_copy(6, 0).wait_send()
    d2d_copy(7, 1).wait_send()
    for pair in range(6):
        ici_copy(pair).wait_send()
    for half in range(2):
        pltpu.make_async_copy(pbuf.at[8 + half], dh_hbm.at[half], out_sem.at[half]).wait()
    out_w.wait()


def solution(mesh):
    groups = mesh.shape["fsdp"]
    tok_spec = P(("dp", "fsdp"), None)

    def local_head(hidden, targets, weight):
        tok_loc, width = hidden.shape
        rows = weight.shape[0]
        tokens = tok_loc * groups
        half = tok_loc // 2
        peers = len(PEERS)
        any_spec = pl.BlockSpec(memory_space=pl.ANY)
        vmem, dma = pltpu.VMEM, pltpu.SemaphoreType.DMA
        loss_row, grad_h, grad_w = pl.pallas_call(
            functools.partial(head_kernel, groups, tokens),
            in_specs=[any_spec] * 3,
            out_specs=[pl.BlockSpec(memory_space=pltpu.VMEM), any_spec, any_spec],
            out_shape=[jax.ShapeDtypeStruct((1, 128), F32), jax.ShapeDtypeStruct((2, half, width), F32), jax.ShapeDtypeStruct((rows, width), F32)],
            scratch_shapes=[
                vmem((groups, 2, half, width), BF16),
                vmem((groups, 2, 1, half), jnp.int32),
                vmem((rows, width), BF16),
                vmem((rows, half), F32),
                vmem((rows, half), BF16),
                vmem((rows, width), F32),
                vmem((10, half, width), F32),
                vmem((8, half, width), F32),
                vmem((2, half, width), F32),
                vmem((2, 2, half, width), F32),
                vmem((groups, 2, 2, 1, half), F32),
                vmem((peers, groups, 2, 2, 1, half), F32),
                vmem((1, half), F32),
                vmem((8, half), F32),
                vmem((1, half), F32),
                vmem((peers, 1, half), F32),
                dma((3,)), dma((2 * peers,)), dma((2 * peers,)), dma((peers,)), dma((peers,)), dma, dma,
                dma((2,)), dma((8,)), dma((6,)), dma((2,)), dma((4,)), dma((peers,)), dma((peers,)), dma((3,)),
            ],
            compiler_params=pltpu.CompilerParams(collective_id=0, has_side_effects=True, vmem_limit_bytes=67_000_000),
            name="head",
        )(hidden.reshape(2, half, width), targets.reshape(2, 1, half), weight)
        return loss_row[0, :1], grad_h.reshape(tok_loc, width), grad_w

    return jax.shard_map(local_head, mesh=mesh, in_specs=(tok_spec, P(("dp", "fsdp")), P("fsdp", None)), out_specs=(P("dp"), tok_spec, tok_spec), check_vma=False)
```

time: 1760 us -> 206 us (0.12)
  waiting for transfers between devices: 1240 us -> 0 us
  matrix products: 241 us -> 0 us
  Pallas kernels: 0 us -> 193 us
  blocking collectives: 114 us -> 0 us
  local copies, waits for them, and re-layouts: 80.1 us -> 10.7 us
  other arithmetic: 39.2 us -> 0 us
  starting transfers between devices: 37.9 us -> 0 us
    ppermute x22 -> x0, waiting for transfers between devices: 1240 us -> none  [the longest x7 929 us: bwd_body(): w_cur = lax.ppermute(w_cur, 'fsdp', ring_pairs)]
    dot_general x31 -> x0, matrix products: 241 us -> none  [the longest x15 117 us: block_logits(): lax.dot_general(hidden, w_blk, (((1,), (1,)), ((), ())), preferred_elemen...]
    pallas_call x0 -> x1, Pallas kernels: none -> 193 us  [local_head(): pl.pallas_call(functools.partial(head_kernel, groups, tokens), in_specs=[...]
    psum x1 -> x0, blocking collectives: 114 us -> none  [local_head(): lax.psum(jnp.sum(log_norm - tgt_logit) / tokens, 'fsdp').reshape(1)]
    while x21 -> x0, local copies, waits for them, and re-layouts: 61.4 us -> none
    reduce_sum x9 -> x0, other arithmetic: 39 us -> none  [the longest x8 38.4 us: fwd_update(): tgt_logit = tgt_logit + jnp.sum(jnp.where(is_target, logits, 0.0), axis=1)]
    ppermute x22 -> x0, starting transfers between devices: 37.9 us -> none  [the longest x7 17.7 us: fwd_body(): w_cur = lax.ppermute(w_cur, 'fsdp', ring_pairs)]
  transfers between devices with their start and end apart: 22 -> 0, of which waited for: 14 -> 0; matrix products, arithmetic and copies ran while one was open for 8% -> 0% of each run, Pallas kernels for 0% -> 0%
where the time goes in v2:
time: 206 us
  Pallas kernels  193 us (94%)
  local copies, waits for them, and re-layouts  10.7 us (5%)
  between operations  2.4 us (1%)
    pallas_call x1, Pallas kernels, local_head(): pl.pallas_call(functools.partial(head_kernel, groups, tokens), in_specs=[...  193 us
    unnamed x2, local copies, waits for them, and re-layouts  10.7 us

profile of v2, /device:TPU:113, one launch (start us, length us, event | category | flops | bytes accessed | tf_op | source)
XLA Modules:
  0.0 206.3 jit_solution(13358453985964670887)
XLA Ops:
  0.6 193.2 %head.1 = (f32[1,128]{1,0:T(1,128)}, f32[2,512,512]{2,1,0:T(8,128)}, f32[4016,512]{1,0:T(8,128)}) custom-call(bf16[2,512,512]{2,1,0:T(8,128)(2,1)} %bitcast.6, s32[2,1,512]{2,1,0:T(1,128)} %bitcast.7, bf16[4016,512]{1,0:T(8,128)(2,1)} %w_hbm.1), custom_call_target="tpu_custom_call" | custom-call | tf_op jit(solution)/shard_map/head/pallas_call | solution.py:322
  194.5 3.1 %copy.10 = f32[1024,512]{1,0:T(8,128)} copy(f32[1024,512]{1,0:T(8,128)} %bitcast.5) | data formatting | bytes 4194304
  197.5 7.6 %copy.11 = f32[4016,512]{1,0:T(8,128)} copy(f32[4016,512]{1,0:T(8,128)} %get-tuple-element.14) | data formatting | bytes 16449536

commit v3 on v2

--- a/solution.py
+++ b/solution.py
@@ -27,11 +27,11 @@
     return [(start, min(ROW_CHUNK, rows - start)) for start in range(0, rows, ROW_CHUNK)]
 
 
-def head_kernel(groups, tokens, hid_hbm, tgt_hbm, w_hbm, loss_ref, dh_hbm, dw_hbm,
+def head_kernel(groups, tokens, hid_hbm, tgt_hbm, w_hbm, loss_ref, dh_hbm, dw_hbm, z_hbm,
                 h_all, t_all, w_ref, z_ref, dz_ref, dw_ref, pbuf, d2d_in, ring_in, fin_in,
                 stat_loc, stat_in, lse_acc, zt_acc, zt_row, zt_in,
                 load_sem, ag_send, ag_recv, tgt_send, tgt_recv, stat_send, stat_recv,
-                d2d_send, d2d_recv, ici_send, ring_recv, fin_recv, zt_send, zt_recv, out_sem):
+                d2d_send, d2d_recv, ici_send, ring_recv, fin_recv, zt_send, zt_recv, out_sem, z_out, z_back):
     chips = groups // CORES
     me = lax.axis_index("fsdp")
     chip = lax.div(me, CORES)
@@ -57,6 +57,17 @@
     dw_ref[...] = jnp.zeros_like(dw_ref)
     lse_acc[...] = jnp.zeros_like(lse_acc)
     zt_acc[...] = jnp.zeros_like(zt_acc)
+
+    def z_store(buf, slot, chunk):
+        start, size = row_chunks(rows)[chunk]
+        return pltpu.make_async_copy(z_ref.at[buf, start:start + size], z_hbm.at[slot, start:start + size], z_out.at[buf, chunk])
+
+    def z_load(buf, slot):
+        return pltpu.make_async_copy(z_hbm.at[slot], z_ref.at[buf], z_back.at[buf])
+
+    num_chunks = len(row_chunks(rows))
+    for chunk, (start, size) in enumerate(row_chunks(rows)):
+        pltpu.make_async_copy(dw_ref.at[start:start + size], z_hbm.at[2 * groups, start:start + size], z_out.at[1, chunk]).start()
     load_h.wait()
     load_t.wait()
     pl.semaphore_wait(barrier, len(PEERS))
@@ -95,21 +106,35 @@
             src_ref=stat_loc.at[block, half], dst_ref=stat_in.at[seen_from(peer), block, half],
             send_sem=stat_send, recv_sem=stat_recv, device_id={"fsdp": dev(*peer)}, device_id_type=MESH)
 
-    def fwd_step(step, carry):
-        grp = lax.div(step, 4)
-        sub = lax.rem(step, 4)
-        flip = lax.div(sub, 2)
-        side = lax.rem(sub, 2)
-        dx = lax.rem(lax.div(grp + 1, 2), 2) * (LEFT + (RIGHT - LEFT) * side) + lax.div(grp, 3) * ACROSS
-        half = side + lax.div(grp, 2) * (1 - lax.div(grp, 3)) * (1 - 2 * side)
-        block = dev(dx, flip)
-
-        @pl.when(step == 2)
+    def fwd_half(buf, block, half):
+        run_max = jnp.full((8, half_toks), -jnp.inf, F32)
+        run_sum = jnp.zeros((8, half_toks), F32)
+        for chunk, (start, size) in enumerate(row_chunks(rows)):
+            sl = slice(start, start + size)
+            z_ref[buf, sl, :] = lax.dot_general(
+                w_ref[sl, :], h_all[block, half], (((1,), (1,)), ((), ())), preferred_element_type=F32)
+            z_grp = z_ref[buf, sl, :].reshape(size // 8, 8, half_toks)
+            new_max = jnp.maximum(run_max, jnp.max(z_grp, axis=0))
+            run_sum = run_sum * jnp.exp(run_max - new_max) + jnp.sum(jnp.exp(z_grp - new_max[None]), axis=0)
+            run_max = new_max
+            z_store(buf, 2 * block + half, chunk).start()
+        tot_max = jnp.max(run_max, axis=0, keepdims=True)
+        stat_loc[block, half, 0] = tot_max
+        stat_loc[block, half, 1] = jnp.sum(run_sum * jnp.exp(run_max - tot_max), axis=0, keepdims=True)
+        for peer in PEERS:
+            stat_copy(peer, block, half).start()
+
+    def fwd_pair(step, carry):
+        grp = lax.div(step, 2)
+        flip = lax.rem(step, 2)
+        mixed = lax.rem(lax.div(grp + 1, 2), 2)
+
+        @pl.when(step == 1)
         def _():
             gather_recv(partner, 0)
             gather_recv(partner, 1)
 
-        @pl.when(step == 4)
+        @pl.when(step == 2)
         def _():
             gather_recv(left, 0)
             gather_copy(left, 0, right).start()
@@ -118,52 +143,54 @@
             gather_copy(right, 1, left).start()
             gather_copy(right, 1, partner).start()
 
-        @pl.when(step == 6)
+        @pl.when(step == 3)
         def _():
             gather_recv((LEFT, 1), 0)
             gather_recv((RIGHT, 1), 1)
 
-        @pl.when(step == 8)
+        @pl.when(step == 4)
         def _():
             gather_recv(left, 1)
             gather_copy(left, 1, partner).start()
             gather_recv(right, 0)
             gather_copy(right, 0, partner).start()
 
-        @pl.when(step == 10)
+        @pl.when(step == 5)
         def _():
             gather_recv((LEFT, 1), 1)
             gather_recv((RIGHT, 1), 0)
 
-        @pl.when(step == 12)
+        @pl.when(step == 6)
         def _():
             gather_recv(across, 0)
             gather_copy(across, 0, partner).start()
             gather_recv(across, 1)
             gather_copy(across, 1, partner).start()
 
-        @pl.when(step == 14)
+        @pl.when(step == 7)
         def _():
             gather_recv((ACROSS, 1), 0)
             gather_recv((ACROSS, 1), 1)
 
-        run_max = jnp.full((8, half_toks), -jnp.inf, F32)
-        run_sum = jnp.zeros((8, half_toks), F32)
-        for start, size in row_chunks(rows):
-            z_ref[start:start + size, :] = lax.dot_general(
-                w_ref[start:start + size, :], h_all[block, half], (((1,), (1,)), ((), ())), preferred_element_type=F32)
-            z_grp = z_ref[start:start + size, :].reshape(size // 8, 8, half_toks)
-            new_max = jnp.maximum(run_max, jnp.max(z_grp, axis=0))
-            run_sum = run_sum * jnp.exp(run_max - new_max) + jnp.sum(jnp.exp(z_grp - new_max[None]), axis=0)
-            run_max = new_max
-        tot_max = jnp.max(run_max, axis=0, keepdims=True)
-        stat_loc[block, half, 0] = tot_max
-        stat_loc[block, half, 1] = jnp.sum(run_sum * jnp.exp(run_max - tot_max), axis=0, keepdims=True)
-        for peer in PEERS:
-            stat_copy(peer, block, half).start()
+        @pl.when(step > 0)
+        def _():
+            for chunk in range(num_chunks):
+                z_store(0, 0, chunk).wait()
+
+        for side in range(2):
+            dx = mixed * (LEFT + (RIGHT - LEFT) * side) + lax.div(grp, 3) * ACROSS
+            half = side + lax.div(grp, 2) * (1 - lax.div(grp, 3)) * (1 - 2 * side)
+            if side == 1:
+                for chunk in range(num_chunks):
+                    z_store(1, 0, chunk).wait()
+            fwd_half(side, dev(dx, flip), half)
         return carry
 
-    lax.fori_loop(0, 2 * groups, fwd_step, 0)
+    lax.fori_loop(0, groups, fwd_pair, 0)
+
+    for buf in range(2):
+        for chunk in range(num_chunks):
+            z_store(buf, 0, chunk).wait()
 
     for peer in PEERS:
         target_copy(peer).wait_recv()
@@ -171,9 +198,9 @@
         src_ref=stat_in, dst_ref=stat_in, send_sem=stat_send, recv_sem=stat_recv, device_id={"fsdp": me}, device_id_type=MESH)
     all_stats.wait_recv()
 
-    def d2d_copy(pair, slot):
-        return pltpu.make_async_remote_copy(
-            src_ref=pbuf.at[slot], dst_ref=d2d_in.at[pair], send_sem=d2d_send.at[slot], recv_sem=d2d_recv.at[pair],
+    def d2d_copy(slot):
+        return pltpu.make_async_remote_copy(
+            src_ref=pbuf.at[slot], dst_ref=d2d_in.at[slot], send_sem=d2d_send.at[slot], recv_sem=d2d_recv.at[slot],
             device_id={"fsdp": dev(*partner)}, device_id_type=MESH)
 
     def ici_copy(pair):
@@ -202,19 +229,16 @@
     inv_tokens = 1.0 / tokens
     log_tokens = jnp.log(jnp.float32(tokens))
 
-    def bwd_step(step, carry):
-        pair = lax.div(step, 2)
-        flip = 1 - lax.rem(step, 2)
+    def pair_block(pair, flip):
         dx = lax.rem(lax.shift_right_logical(jnp.int32(DX_CODE), 2 * pair), 4)
         half = lax.rem(lax.shift_right_logical(jnp.int32(HALF_CODE), 2 * pair), 4)
-        block = dev(dx, flip)
-        slot = flip * lax.rem(pair, 2) + (1 - flip) * (2 + pair)
-
-        for pair_s in range(2, 8):
-            @pl.when(step == 2 * pair_s)
-            def _():
-                d2d_copy(pair_s - 2, pair_s % 2).wait_send()
-
+        return dev(dx, flip), half
+
+    def z_slot(pair, flip):
+        block, half = pair_block(pair, flip)
+        return 2 * block + half
+
+    def bwd_half(buf, slot, block, half):
         maxes = [stat_loc[block, half, 0]] + [stat_in[i, block, half, 0] for i in range(len(PEERS))]
         sums = [stat_loc[block, half, 1]] + [stat_in[i, block, half, 1] for i in range(len(PEERS))]
         tot_max = functools.reduce(jnp.maximum, maxes)
@@ -227,8 +251,7 @@
         h_tile = h_all.at[block, half]
         for idx, (start, size) in enumerate(row_chunks(rows)):
             sl = slice(start, start + size)
-            z_ref[sl, :] = lax.dot_general(w_ref[sl, :], h_tile[...], (((1,), (1,)), ((), ())), preferred_element_type=F32)
-            z = z_ref[sl, :]
+            z = z_ref[buf, sl, :]
             mask = (lax.broadcasted_iota(jnp.int32, (size, half_toks), 0) + start) == tgt
             prob = jnp.exp(z - shift)
             dz_ref[sl, :] = jnp.where(mask, prob - inv_tokens, prob).astype(BF16)
@@ -241,15 +264,34 @@
                 pbuf[slot] += dh_part
         zt_acc[...] = zt_sum
 
+    def bwd_pair(pair, carry):
+        odd = lax.rem(pair, 2)
+
+        @pl.when(pair >= 2)
+        def _():
+            d2d_copy(odd).wait_send()
+
+        @pl.when(pair >= 1)
+        def _():
+            z_load(0, 0).wait()
+
+        block, half = pair_block(pair, 1)
+        bwd_half(0, odd, block, half)
+        d2d_copy(odd).start()
+        z_load(0, z_slot(lax.rem(pair + 1, groups), 1)).start()
+        z_load(1, 0).wait()
+        block, half = pair_block(pair, 0)
+        bwd_half(1, 2 + pair, block, half)
+
+        @pl.when(pair < groups - 1)
+        def _():
+            z_load(1, z_slot(pair + 1, 0)).start()
+
+        d2d_copy(odd).wait_recv()
         for pair_s in range(8):
-            @pl.when(step == 2 * pair_s)
+            @pl.when(pair == pair_s)
             def _():
-                d2d_copy(pair_s, pair_s % 2).start()
-
-            @pl.when(step == 2 * pair_s + 1)
-            def _():
-                d2d_copy(pair_s, pair_s % 2).wait_recv()
-                sources = [d2d_in.at[pair_s]]
+                sources = [d2d_in.at[pair_s % 2]]
                 dx_s, half_s = PAIR_DX[pair_s], PAIR_HALF[pair_s]
                 if (dx_s, half_s) == (RIGHT, 0):
                     ici_copy(0).wait_recv()
@@ -269,7 +311,8 @@
                     ici_copy(pair_s).start()
         return carry
 
-    lax.fori_loop(0, 2 * groups, bwd_step, 0)
+    z_load(1, z_slot(0, 0)).start()
+    lax.fori_loop(0, groups, bwd_pair, 0)
 
     out_w = pltpu.make_async_copy(dw_ref, dw_hbm, out_sem.at[2])
     out_w.start()
@@ -298,8 +341,9 @@
     for peer in PEERS:
         target_copy(peer).wait_send()
     all_stats.wait_send()
-    d2d_copy(6, 0).wait_send()
-    d2d_copy(7, 1).wait_send()
+    d2d_copy(0).wait_send()
+    d2d_copy(1).wait_send()
+    z_load(0, 0).wait()
     for pair in range(6):
         ici_copy(pair).wait_send()
     for half in range(2):
@@ -319,20 +363,20 @@
         peers = len(PEERS)
         any_spec = pl.BlockSpec(memory_space=pl.ANY)
         vmem, dma = pltpu.VMEM, pltpu.SemaphoreType.DMA
-        loss_row, grad_h, grad_w = pl.pallas_call(
+        loss_row, grad_h, grad_w, _ = pl.pallas_call(
             functools.partial(head_kernel, groups, tokens),
             in_specs=[any_spec] * 3,
-            out_specs=[pl.BlockSpec(memory_space=pltpu.VMEM), any_spec, any_spec],
-            out_shape=[jax.ShapeDtypeStruct((1, 128), F32), jax.ShapeDtypeStruct((2, half, width), F32), jax.ShapeDtypeStruct((rows, width), F32)],
+            out_specs=[pl.BlockSpec(memory_space=pltpu.VMEM), any_spec, any_spec, any_spec],
+            out_shape=[jax.ShapeDtypeStruct((1, 128), F32), jax.ShapeDtypeStruct((2, half, width), F32), jax.ShapeDtypeStruct((rows, width), F32), jax.ShapeDtypeStruct((2 * groups + 1, rows, half), F32)],
             scratch_shapes=[
                 vmem((groups, 2, half, width), BF16),
                 vmem((groups, 2, 1, half), jnp.int32),
                 vmem((rows, width), BF16),
-                vmem((rows, half), F32),
+                vmem((2, rows, half), F32),
                 vmem((rows, half), BF16),
                 vmem((rows, width), F32),
                 vmem((10, half, width), F32),
-                vmem((8, half, width), F32),
+                vmem((2, half, width), F32),
                 vmem((2, half, width), F32),
                 vmem((2, 2, half, width), F32),
                 vmem((groups, 2, 2, 1, half), F32),
@@ -342,7 +386,8 @@
                 vmem((1, half), F32),
                 vmem((peers, 1, half), F32),
                 dma((3,)), dma((2 * peers,)), dma((2 * peers,)), dma((peers,)), dma((peers,)), dma, dma,
-                dma((2,)), dma((8,)), dma((6,)), dma((2,)), dma((4,)), dma((peers,)), dma((peers,)), dma((3,)),
+                dma((2,)), dma((2,)), dma((6,)), dma((2,)), dma((4,)), dma((peers,)), dma((peers,)), dma((3,)),
+                dma((2, len(row_chunks(rows)))), dma((2,)),
             ],
             compiler_params=pltpu.CompilerParams(collective_id=0, has_side_effects=True, vmem_limit_bytes=67_000_000),
             name="head",

time: 206 us -> 175 us (0.85)
  Pallas kernels: 193 us -> 162 us
    pallas_call x1, Pallas kernels: 193 us -> 162 us  [local_head(): pl.pallas_call(functools.partial(head_kernel, groups, tokens), in_specs=[...]
where the time goes in v3:
time: 175 us
  Pallas kernels  162 us (93%)
  local copies, waits for them, and re-layouts  10.7 us (6%)
  between operations  2.4 us (1%)
    pallas_call x1, Pallas kernels, local_head(): pl.pallas_call(functools.partial(head_kernel, groups, tokens), in_specs=[...  162 us
    unnamed x2, local copies, waits for them, and re-layouts  10.7 us

profile of v3, /device:TPU:113, one launch (start us, length us, event | category | flops | bytes accessed | tf_op | source)
XLA Modules:
  0.0 175.1 jit_solution(17627702024053810945)
XLA Ops:
  0.6 162.0 %head.1 = (f32[1,128]{1,0:T(1,128)}, f32[2,512,512]{2,1,0:T(8,128)}, f32[4016,512]{1,0:T(8,128)}, f32[17,4016,512]{2,1,0:T(8,128)}) custom-call(bf16[2,512,512]{2,1,0:T(8,128)(2,1)} %bitcast.6, s32[2,1,512]{2,1,0:T(1,128)} %bitcast.7, bf16[4016,512]{1,0:T(8,128)(2,1)} %w_hbm.1), custom_call_target="tpu_custom_call" | custom-call | tf_op jit(solution)/shard_map/head/pallas_call | solution.py:366
  163.3 3.1 %copy.10 = f32[1024,512]{1,0:T(8,128)} copy(f32[1024,512]{1,0:T(8,128)} %bitcast.5) | data formatting | bytes 4194304
  166.3 7.6 %copy.11 = f32[4016,512]{1,0:T(8,128)} copy(f32[4016,512]{1,0:T(8,128)} %get-tuple-element.14) | data formatting | bytes 16449536

commit v4 on v0

v4 whole, which is shorter than its diff:
```python
import functools

import jax
import jax.numpy as jnp
from jax import lax
from jax.experimental import pallas as pl
from jax.experimental.pallas import tpu as pltpu
from jax.sharding import PartitionSpec as P

F32 = jnp.float32
BF16 = jnp.bfloat16
MESH = pl.DeviceIdType.MESH
CORES = 2
FWD_CHUNK = 512
BWD_CHUNK = 1008
TAIL_ROWS = 512

LEFT, RIGHT, ACROSS = 3, 1, 2
OWN, PARTNER = (0, 0), (0, 1)
PEERS = [PARTNER, (LEFT, 0), (LEFT, 1), (RIGHT, 0), (RIGHT, 1), (ACROSS, 0), (ACROSS, 1)]
PEER_SLOT = {peer: slot for slot, peer in enumerate(PEERS)}

def tile_id(kind, flip, j):
    if kind == "mixed":
        return 4 + 2 * flip + 4 * (j // 2) + j % 2
    return {"own": 0, "across": 12}[kind] + 2 * flip + j


def place(owner, quarter):
    dx, flip = owner
    if dx in (LEFT, RIGHT):
        return tile_id("mixed", flip, quarter), 0 if dx == RIGHT else 1
    return tile_id("own" if dx == 0 else "across", flip, quarter // 2), quarter % 2


PAIRS = [("across", 0), ("across", 1)] + [("mixed", j) for j in range(4)] + [("own", 0), ("own", 1)]
PAIR_CODE = sum(tile_id(kind, 0, j) << (4 * q) for q, (kind, j) in enumerate(PAIRS))


def chunks(rows, step):
    return [(start, min(step, rows - start)) for start in range(0, rows, step)]


def head_kernel(groups, tokens, hid_hbm, tgt_hbm, w_hbm, loss_ref, dh_hbm, dw_hbm, dz_hbm, htail_hbm, z_hbm,
                h_all, t_all, w_ref, z_ref, dz_ref, dw_ref, pbuf, d2d_in, ring_in, fin_in,
                stat_loc, stat_in, lse_acc, zt_acc, zt_row, zt_in,
                load_sem, ag_send, ag_recv, tgt_send, tgt_recv, stat_send, stat_recv,
                d2d_send, d2d_recv, ici_send, ring_recv, fin_recv, zt_send, zt_recv, out_sem, z_out, z_back):
    chips = groups // CORES
    me = lax.axis_index("fsdp")
    chip = lax.div(me, CORES)
    core = lax.rem(me, CORES)
    rows, width = w_ref.shape
    tile = h_all.shape[1]
    quarter_toks = tile // 2
    parts = [pl.ds(0, quarter_toks), pl.ds(quarter_toks, quarter_toks)]
    left, right, across = (LEFT, 0), (RIGHT, 0), (ACROSS, 0)

    def dev(dx, flip):
        return lax.rem(chip + dx, chips) * CORES + lax.rem(core + flip, CORES)

    def seen_from(peer):
        return PEER_SLOT[((chips - peer[0]) % chips, peer[1])]

    loads = [pltpu.make_async_copy(hid_hbm.at[j], h_all.at[tile_id("own", 0, j)], load_sem.at[j]) for j in range(2)]
    loads.append(pltpu.make_async_copy(tgt_hbm, t_all.at[me], load_sem.at[2]))
    load_w = pltpu.make_async_copy(w_hbm, w_ref, load_sem.at[3])
    for load in loads:
        load.start()
    load_w.start()
    barrier = pltpu.get_barrier_semaphore()
    for peer in PEERS:
        pl.semaphore_signal(barrier, inc=1, device_id={"fsdp": dev(*peer)}, device_id_type=MESH)
    dw_ref[...] = jnp.zeros_like(dw_ref)
    lse_acc[...] = jnp.zeros_like(lse_acc)
    zt_acc[...] = jnp.zeros_like(zt_acc)

    fwd_chunks = chunks(rows, FWD_CHUNK)

    def z_store(buf, slot, chunk):
        start, size = fwd_chunks[chunk]
        return pltpu.make_async_copy(z_ref.at[buf, start:start + size], z_hbm.at[slot, start:start + size], z_out.at[buf, chunk])

    def z_load(buf, slot):
        return pltpu.make_async_copy(z_hbm.at[slot], z_ref.at[buf], z_back.at[buf])

    for chunk, (start, size) in enumerate(fwd_chunks):
        pltpu.make_async_copy(dw_ref.at[start:start + size], z_hbm.at[2 * groups, start:start + size], z_out.at[1, chunk]).start()
    for load in loads:
        load.wait()
    pl.semaphore_wait(barrier, len(PEERS))

    def gather_copy(owner, quarter, to):
        src_tile, src_part = place(owner, quarter)
        as_seen = ((owner[0] - to[0]) % chips, (owner[1] + to[1]) % CORES)
        dst_tile, dst_part = place(as_seen, quarter)
        idx = PEER_SLOT[as_seen] * 4 + quarter
        return pltpu.make_async_remote_copy(
            src_ref=h_all.at[src_tile, parts[src_part]], dst_ref=h_all.at[dst_tile, parts[dst_part]],
            send_sem=ag_send.at[idx], recv_sem=ag_recv.at[idx], device_id={"fsdp": dev(*to)}, device_id_type=MESH)

    def gather_recv(owner, quarter):
        dst_tile, dst_part = place(owner, quarter)
        idx = PEER_SLOT[owner] * 4 + quarter
        dst = h_all.at[dst_tile, parts[dst_part]]
        pltpu.make_async_remote_copy(
            src_ref=dst, dst_ref=dst, send_sem=ag_send.at[idx], recv_sem=ag_recv.at[idx],
            device_id={"fsdp": me}, device_id_type=MESH).wait_recv()

    for quarter in range(4):
        for to in (right, left, PARTNER):
            gather_copy(OWN, quarter, to).start()

    def target_copy(peer):
        slot = seen_from(peer)
        return pltpu.make_async_remote_copy(
            src_ref=t_all.at[me], dst_ref=t_all.at[me], send_sem=tgt_send.at[slot], recv_sem=tgt_recv.at[slot],
            device_id={"fsdp": dev(*peer)}, device_id_type=MESH)

    for peer in PEERS:
        target_copy(peer).start()
    load_w.wait()

    def pieces(tid):
        grp = lax.div(tid, 4)
        flip = lax.rem(lax.div(tid, 2), 2)
        j = lax.rem(tid, 2)
        mixed = lax.rem(lax.div(grp + 1, 2), 2)
        out = []
        for part in range(2):
            dx = mixed * (RIGHT, LEFT)[part] + lax.div(grp, 3) * ACROSS
            quarter = mixed * (2 * lax.div(grp, 2) + j) + (1 - mixed) * (2 * j + part)
            out.append((dev(dx, flip), quarter))
        return out

    def stat_copy(peer, block, quarter):
        return pltpu.make_async_remote_copy(
            src_ref=stat_loc.at[block, quarter], dst_ref=stat_in.at[seen_from(peer), block, quarter],
            send_sem=stat_send, recv_sem=stat_recv, device_id={"fsdp": dev(*peer)}, device_id_type=MESH)

    def fwd_tile(buf, tid):
        run_max = jnp.full((8, tile), -jnp.inf, F32)
        run_sum = jnp.zeros((8, tile), F32)
        for chunk, (start, size) in enumerate(fwd_chunks):
            sl = slice(start, start + size)
            z_ref[buf, sl, :] = lax.dot_general(
                w_ref[sl, :], h_all[tid], (((1,), (1,)), ((), ())), preferred_element_type=F32)
            z_grp = z_ref[buf, sl, :].reshape(size // 8, 8, tile)
            new_max = jnp.maximum(run_max, jnp.max(z_grp, axis=0))
            run_sum = run_sum * jnp.exp(run_max - new_max) + jnp.sum(jnp.exp(z_grp - new_max[None]), axis=0)
            run_max = new_max
            z_store(buf, tid, chunk).start()
        tot_max = jnp.max(run_max, axis=0, keepdims=True)
        tot_sum = jnp.sum(run_sum * jnp.exp(run_max - tot_max), axis=0, keepdims=True)
        for part, (block, quarter) in enumerate(pieces(tid)):
            lanes = slice(part * quarter_toks, (part + 1) * quarter_toks)
            stat_loc[block, quarter, 0] = tot_max[:, lanes]
            stat_loc[block, quarter, 1] = tot_sum[:, lanes]
        for block, quarter in pieces(tid):
            for peer in PEERS:
                stat_copy(peer, block, quarter).start()

    def fwd_pair(step, carry):
        @pl.when(step == 1)
        def _():
            for quarter in range(4):
                gather_recv(PARTNER, quarter)

        for late in range(2):
            @pl.when(step == 2 + 2 * late)
            def _():
                for quarter in (2 * late, 2 * late + 1):
                    for owner in (left, right):
                        gather_recv(owner, quarter)
                        if late == 0 and owner == left:
                            gather_copy(left, quarter, right).start()
                        if late == 1 and owner == right:
                            gather_copy(right, quarter, left).start()
                        gather_copy(owner, quarter, PARTNER).start()

            @pl.when(step == 3 + 2 * late)
            def _():
                for quarter in (2 * late, 2 * late + 1):
                    gather_recv((LEFT, 1), quarter)
                    gather_recv((RIGHT, 1), quarter)

        @pl.when(step == 6)
        def _():
            for quarter in range(4):
                gather_recv(across, quarter)
                gather_copy(across, quarter, PARTNER).start()

        @pl.when(step == 7)
        def _():
            for quarter in range(4):
                gather_recv((ACROSS, 1), quarter)

        @pl.when(step > 0)
        def _():
            for chunk in range(len(fwd_chunks)):
                z_store(0, 0, chunk).wait()

        fwd_tile(0, 2 * step)
        for chunk in range(len(fwd_chunks)):
            z_store(1, 0, chunk).wait()
        fwd_tile(1, 2 * step + 1)
        return carry

    lax.fori_loop(0, groups, fwd_pair, 0)

    for buf in range(2):
        for chunk in range(len(fwd_chunks)):
            z_store(buf, 0, chunk).wait()

    def pair_tile(pair, flip):
        return lax.rem(lax.shift_right_logical(jnp.int32(PAIR_CODE), 4 * pair), 16) + 2 * flip

    z_load(1, pair_tile(0, 0)).start()
    for peer in PEERS:
        target_copy(peer).wait_recv()
    all_stats = pltpu.make_async_remote_copy(
        src_ref=stat_in, dst_ref=stat_in, send_sem=stat_send, recv_sem=stat_recv, device_id={"fsdp": me}, device_id_type=MESH)
    all_stats.wait_recv()

    def d2d_copy(slot):
        return pltpu.make_async_remote_copy(
            src_ref=pbuf.at[slot], dst_ref=d2d_in.at[slot], send_sem=d2d_send.at[slot], recv_sem=d2d_recv.at[slot],
            device_id={"fsdp": dev(*PARTNER)}, device_id_type=MESH)

    def ici_copy(pair, part):
        kind, j = PAIRS[pair]
        if kind == "across":
            dst, recv = ring_in.at[part, j], ring_recv.at[part * 2 + j]
        else:
            dst, recv = fin_in.at[part, j // 2, parts[j % 2]], fin_recv.at[part * 4 + j]
        return pltpu.make_async_remote_copy(
            src_ref=pbuf.at[2 + pair % 4, parts[part]], dst_ref=dst, send_sem=ici_send.at[(pair % 4) * 2 + part], recv_sem=recv,
            device_id={"fsdp": dev(*(right, left)[part])}, device_id_type=MESH)

    def wait_ici_sends(slot):
        for part in range(2):
            pltpu.make_async_remote_copy(
                src_ref=pbuf.at[2 + slot, parts[part]], dst_ref=ring_in.at[0, 0], send_sem=ici_send.at[slot * 2 + part],
                recv_sem=ring_recv.at[0], device_id={"fsdp": me}, device_id_type=MESH).wait_send()

    def add_into(slot, base, count, sources):
        def body(i, carry):
            off = pl.multiple_of(i * 64, 64)
            sl = pl.ds(base + off, 64)
            tot = pbuf[slot, sl, :]
            for src in sources:
                tot = tot + src[pl.ds(off, 64), :]
            pbuf[slot, sl, :] = tot
            return carry
        lax.fori_loop(0, count // 64, body, 0)

    inv_tokens = 1.0 / tokens
    log_tokens = jnp.log(jnp.float32(tokens))
    bwd_chunks = chunks(rows, BWD_CHUNK)

    def bwd_tile(buf, slot, tid, with_dw):
        where = pieces(tid)

        stats = [stat_loc] + [stat_in.at[i] for i in range(len(PEERS))]
        maxes, sums = [
            [jnp.concatenate([ref[block, quarter, kind] for block, quarter in where], axis=1) for ref in stats] for kind in range(2)]
        tot_max = functools.reduce(jnp.maximum, maxes)
        tot_sum = sum(s * jnp.exp(m - tot_max) for m, s in zip(maxes, sums))
        lse = tot_max + jnp.log(tot_sum)
        lse_acc[...] += lse
        shift = lse + log_tokens
        tgt = jnp.concatenate([t_all[block, quarter] for block, quarter in where], axis=1) - me * rows
        zt_sum = zt_acc[...]
        for idx, (start, size) in enumerate(bwd_chunks):
            sl = slice(start, start + size)
            z = z_ref[buf, sl, :]
            mask = (lax.broadcasted_iota(jnp.int32, (size, tile), 0) + start) == tgt
            prob = jnp.exp(z - shift)
            dz_ref[buf, sl, :] = jnp.where(mask, prob - inv_tokens, prob).astype(BF16)
            zt_sum += jnp.sum(jnp.where(mask, z, 0.0).reshape(size // 8, 8, tile), axis=0)
            if with_dw:
                dw_ref[sl, :] += jnp.dot(dz_ref[buf, sl, :], h_all[tid], preferred_element_type=F32)
            dh_part = lax.dot_general(dz_ref[buf, sl, :], w_ref[sl, :], (((0,), (0,)), ((), ())), preferred_element_type=F32)
            if idx == 0:
                pbuf[slot] = dh_part
            else:
                pbuf[slot] += dh_part
        zt_acc[...] = zt_sum

    def finish_pair(pair):
        kind, j = PAIRS[pair]
        slot = 2 + pair % 4
        if kind == "own":
            for part in range(2):
                for q in range(2):
                    ici_copy(2 + 2 * j + q, part).wait_recv()
            add_into(slot, 0, tile, [d2d_in.at[pair % 2], fin_in.at[0, j], fin_in.at[1, j]])
            pltpu.make_async_copy(pbuf.at[slot], dh_hbm.at[j], out_sem.at[j]).start()
            return
        for part in range(2):
            sources = [d2d_in.at[pair % 2, parts[part]]]
            if kind == "mixed" and j % 2 == part:
                ici_copy(j // 2, part).wait_recv()
                sources.append(ring_in.at[part, j // 2])
            add_into(slot, part * quarter_toks, quarter_toks, sources)
            ici_copy(pair, part).start()

    def bwd_pair(pair, carry):
        odd = lax.rem(pair, 2)

        @pl.when(pair >= 2)
        def _():
            d2d_copy(odd).wait_send()

        @pl.when(pair >= 4)
        def _():
            wait_ici_sends(pair - 4)

        @pl.when(pair >= 1)
        def _():
            z_load(0, 0).wait()

        bwd_tile(0, odd, pair_tile(pair, 1), True)
        d2d_copy(odd).start()
        z_load(0, pair_tile(pair + 1, 1)).start()
        z_load(1, 0).wait()
        bwd_tile(1, 2 + lax.rem(pair, 4), pair_tile(pair, 0), True)
        z_load(1, pair_tile(pair + 1, 0)).start()
        d2d_copy(odd).wait_recv()
        for pair_s in range(len(PAIRS) - 1):
            @pl.when(pair == pair_s)
            def _():
                finish_pair(pair_s)
        return carry

    last = len(PAIRS) - 1
    lax.fori_loop(0, last, bwd_pair, 0)

    outs = [pltpu.make_async_copy(dw_ref, dw_hbm, out_sem.at[2])]
    outs += [pltpu.make_async_copy(h_all.at[tile_id("own", 1 - i, 1)], htail_hbm.at[i], out_sem.at[3 + i]) for i in range(2)]
    for out in outs:
        out.start()
    d2d_copy(last % 2).wait_send()
    wait_ici_sends(last - 4)
    for buf in range(2):
        z_load(buf, 0).wait()
        bwd_tile(buf, (last % 2, 2 + last % 4)[buf], tile_id("own", 1 - buf, 1), False)
        outs.append(pltpu.make_async_copy(dz_ref.at[buf], dz_hbm.at[buf], out_sem.at[5 + buf]))
        outs[-1].start()
        if buf == 0:
            d2d_copy(last % 2).start()

    zt_row[...] = jnp.sum(zt_acc[...], axis=0, keepdims=True)

    def zt_copy(peer):
        slot = seen_from(peer)
        return pltpu.make_async_remote_copy(
            src_ref=zt_row, dst_ref=zt_in.at[slot], send_sem=zt_send.at[slot], recv_sem=zt_recv.at[slot],
            device_id={"fsdp": dev(*peer)}, device_id_type=MESH)

    for peer in PEERS:
        zt_copy(peer).start()
    d2d_copy(last % 2).wait_recv()
    finish_pair(last)
    for peer in PEERS:
        zt_copy(peer).wait()
    tot = lse_acc[...] - zt_row[...]
    for i in range(len(PEERS)):
        tot = tot - zt_in[i]
    loss_ref[...] = jnp.broadcast_to(jnp.sum(tot, axis=1, keepdims=True) * inv_tokens, loss_ref.shape)

    for owner, quarter, to in (
            [(OWN, q, to) for q in range(4) for to in (right, left, PARTNER)]
            + [(left, q, right) for q in (0, 1)] + [(right, q, left) for q in (2, 3)]
            + [(side, q, PARTNER) for side in (left, right, across) for q in range(4)]):
        gather_copy(owner, quarter, to).wait_send()
    for peer in PEERS:
        target_copy(peer).wait_send()
    all_stats.wait_send()
    for slot in range(2):
        d2d_copy(slot).wait_send()
    for pair in (4, 5):
        wait_ici_sends(pair % 4)
    for j in range(2):
        pltpu.make_async_copy(pbuf.at[2 + (6 + j) % 4], dh_hbm.at[j], out_sem.at[j]).wait()
    for out in outs:
        out.wait()


def tail_kernel(dw_ref, dz_ref, h_ref, dh_ref, dw_out, dh_out):
    tot = dw_ref[...]
    for i in range(2):
        tot = tot + jnp.dot(dz_ref[i], h_ref[i], preferred_element_type=F32)
    dw_out[...] = tot
    dh_out[...] = dh_ref[...]


def solution(mesh):
    groups = mesh.shape["fsdp"]
    tok_spec = P(("dp", "fsdp"), None)

    def local_head(hidden, targets, weight):
        tok_loc, width = hidden.shape
        rows = weight.shape[0]
        tokens = tok_loc * groups
        tile, quarter = tok_loc // 2, tok_loc // 4
        peers = len(PEERS)
        any_spec = pl.BlockSpec(memory_space=pl.ANY)
        vmem, dma = pltpu.VMEM, pltpu.SemaphoreType.DMA
        shape = jax.ShapeDtypeStruct
        loss_row, grad_h, dw_part, dz_tail, h_tail, _ = pl.pallas_call(
            functools.partial(head_kernel, groups, tokens),
            in_specs=[any_spec] * 3,
            out_specs=[pl.BlockSpec(memory_space=pltpu.VMEM)] + [any_spec] * 5,
            out_shape=[
                shape((1, 128), F32), shape((2, tile, width), F32), shape((rows, width), F32), shape((2, rows, tile), BF16),
                shape((2, tile, width), BF16), shape((2 * groups + 1, rows, tile), F32)],
            scratch_shapes=[
                vmem((2 * groups, tile, width), BF16),
                vmem((groups, 4, 1, quarter), jnp.int32),
                vmem((rows, width), BF16),
                vmem((2, rows, tile), F32),
                vmem((2, rows, tile), BF16),
                vmem((rows, width), F32),
                vmem((6, tile, width), F32),
                vmem((2, tile, width), F32),
                vmem((2, 2, quarter, width), F32),
                vmem((2, 2, tile, width), F32),
                vmem((groups, 4, 2, 1, quarter), F32),
                vmem((peers, groups, 4, 2, 1, quarter), F32),
                vmem((1, tile), F32),
                vmem((8, tile), F32),
                vmem((1, tile), F32),
                vmem((peers, 1, tile), F32),
                dma((4,)), dma((4 * peers,)), dma((4 * peers,)), dma((peers,)), dma((peers,)), dma, dma,
                dma((2,)), dma((2,)), dma((8,)), dma((4,)), dma((8,)), dma((peers,)), dma((peers,)), dma((7,)),
                dma((2, len(chunks(rows, FWD_CHUNK)))), dma((2,)),
            ],
            compiler_params=pltpu.CompilerParams(collective_id=0, has_side_effects=True, vmem_limit_bytes=67_000_000),
            name="head",
        )(hidden.reshape(2, tile, width), targets.reshape(4, 1, quarter), weight)
        steps = pl.cdiv(rows, TAIL_ROWS)
        row_spec = pl.BlockSpec((TAIL_ROWS, width), lambda i: (i, 0))
        dh_spec = pl.BlockSpec((tok_loc // steps, width), lambda i: (i, 0))
        grad_w, grad_h = pl.pallas_call(
            tail_kernel,
            grid=(steps,),
            in_specs=[row_spec, pl.BlockSpec((2, TAIL_ROWS, tile), lambda i: (0, i, 0)),
                      pl.BlockSpec((2, tile, width), lambda i: (0, 0, 0)), dh_spec],
            out_specs=[row_spec, dh_spec],
            out_shape=[shape((rows, width), F32), shape((tok_loc, width), F32)],
            name="tail",
        )(dw_part, dz_tail, h_tail, grad_h.reshape(tok_loc, width))
        return loss_row[0, :1], grad_h, grad_w

    return jax.shard_map(local_head, mesh=mesh, in_specs=(tok_spec, P(("dp", "fsdp")), P("fsdp", None)), out_specs=(P("dp"), tok_spec, tok_spec), check_vma=False)
```

time: 1760 us -> 169 us (0.10)
  waiting for transfers between devices: 1240 us -> 0 us
  matrix products: 241 us -> 0 us
  Pallas kernels: 0 us -> 167 us
  blocking collectives: 114 us -> 0 us
  local copies, waits for them, and re-layouts: 80.1 us -> 0.01 us
  other arithmetic: 39.2 us -> 0 us
  starting transfers between devices: 37.9 us -> 0 us
    ppermute x22 -> x0, waiting for transfers between devices: 1240 us -> none  [the longest x7 929 us: bwd_body(): w_cur = lax.ppermute(w_cur, 'fsdp', ring_pairs)]
    dot_general x31 -> x0, matrix products: 241 us -> none  [the longest x15 117 us: block_logits(): lax.dot_general(hidden, w_blk, (((1,), (1,)), ((), ())), preferred_elemen...]
    pallas_call x0 -> x2, Pallas kernels: none -> 167 us  [the longest x1 153 us: local_head(): pl.pallas_call(functools.partial(head_kernel, groups, tokens), in_specs=[...]
    psum x1 -> x0, blocking collectives: 114 us -> none  [local_head(): lax.psum(jnp.sum(log_norm - tgt_logit) / tokens, 'fsdp').reshape(1)]
    while x21 -> x0, local copies, waits for them, and re-layouts: 61.4 us -> none
    reduce_sum x9 -> x0, other arithmetic: 39 us -> none  [the longest x8 38.4 us: fwd_update(): tgt_logit = tgt_logit + jnp.sum(jnp.where(is_target, logits, 0.0), axis=1)]
    ppermute x22 -> x0, starting transfers between devices: 37.9 us -> none  [the longest x7 17.7 us: fwd_body(): w_cur = lax.ppermute(w_cur, 'fsdp', ring_pairs)]
    unnamed x13 -> x2, local copies, waits for them, and re-layouts: 18.7 us -> 0.01 us
  transfers between devices with their start and end apart: 22 -> 0, of which waited for: 14 -> 0; matrix products, arithmetic and copies ran while one was open for 8% -> 0% of each run, Pallas kernels for 0% -> 0%
where the time goes in v4:
time: 169 us
  Pallas kernels  167 us (99%)
  between operations  1.81 us (1%)
    pallas_call x1, Pallas kernels, local_head(): pl.pallas_call(functools.partial(head_kernel, groups, tokens), in_specs=[...  153 us
    pallas_call x1, Pallas kernels, local_head(): pl.pallas_call(tail_kernel, grid=(steps,), in_specs=[row_spec, pl.BlockSp...  14.3 us

profile of v4, /device:TPU:113, one launch (start us, length us, event | category | flops | bytes accessed | tf_op | source)
XLA Modules:
  0.0 168.9 jit_solution(11370432735075481181)
XLA Ops:
  0.6 152.8 %head.1 = (f32[1,128]{1,0:T(1,128)}, f32[2,512,512]{2,1,0:T(8,128)}, f32[4016,512]{1,0:T(8,128)}, bf16[2,4016,512]{2,1,0:T(8,128)(2,1)}, bf16[2,512,512]{2,1,0:T(8,128)(2,1)}, /*index=5*/f32[17,4016,512]{2,1,0:T(8,128)}) custom-call(bf16[2,512,512]{2,1,0:T(8,128)(2,1)} %bitcast.6, s32[4,1,256]{2,1,0:T(1,128)} %bitcast.7, bf16[4016,512]{1,0:T(8,128)(2,1)} %w_hbm.1), custom_call_target="tpu_custom_call" | custom-call | tf_op jit(solution)/shard_map/head/pallas_call | solution.py:411
  153.5 0.0 copy-start
  153.5 14.3 %tail.1 = (f32[4016,512]{1,0:T(8,128)}, f32[1024,512]{1,0:T(8,128)}) custom-call(f32[4016,512]{1,0:T(8,128)} %get-tuple-element.11.dw_ref, bf16[2,4016,512]{2,1,0:T(8,128)(2,1)} %get-tuple-element.12.dz_ref, bf16[2,512,512]{2,1,0:T(8,128)(2,1)} %get-tuple-element.13.h_ref, f32[1024,512]{1,0:T(8,128)} %bitcast.5), custom_call_target="tpu_custom_call" | custom-call | tf_op jit(solution)/shard_map/tail/pallas_call | solution.py:445
  167.7 0.0 copy-done
Async XLA Ops:
  153.5 14.3 %copy-start = (f32[1,128]{1,0:T(1,128)S(1)}, f32[1,128]{1,0:T(1,128)}, u32[]{:S(2)}) copy-start(f32[1,128]{1,0:T(1,128)} %get-tuple-element.10) | copy-start | bytes 1540

commit v5 on v4

--- a/solution.py
+++ b/solution.py
@@ -11,9 +11,9 @@
 BF16 = jnp.bfloat16
 MESH = pl.DeviceIdType.MESH
 CORES = 2
-FWD_CHUNK = 512
-BWD_CHUNK = 1008
-TAIL_ROWS = 512
+CHUNK = 1008
+GROUP = 112
+COPY_ROWS = 512
 
 LEFT, RIGHT, ACROSS = 3, 1, 2
 OWN, PARTNER = (0, 0), (0, 1)
@@ -41,7 +41,7 @@
     return [(start, min(step, rows - start)) for start in range(0, rows, step)]
 
 
-def head_kernel(groups, tokens, hid_hbm, tgt_hbm, w_hbm, loss_ref, dh_hbm, dw_hbm, dz_hbm, htail_hbm, z_hbm,
+def head_kernel(groups, tokens, hid_hbm, tgt_hbm, w_hbm, loss_ref, dh_hbm, dw_hbm, z_hbm,
                 h_all, t_all, w_ref, z_ref, dz_ref, dw_ref, pbuf, d2d_in, ring_in, fin_in,
                 stat_loc, stat_in, lse_acc, zt_acc, zt_row, zt_in,
                 load_sem, ag_send, ag_recv, tgt_send, tgt_recv, stat_send, stat_recv,
@@ -75,16 +75,16 @@
     lse_acc[...] = jnp.zeros_like(lse_acc)
     zt_acc[...] = jnp.zeros_like(zt_acc)
 
-    fwd_chunks = chunks(rows, FWD_CHUNK)
+    row_chunks = chunks(rows, CHUNK)
 
     def z_store(buf, slot, chunk):
-        start, size = fwd_chunks[chunk]
+        start, size = row_chunks[chunk]
         return pltpu.make_async_copy(z_ref.at[buf, start:start + size], z_hbm.at[slot, start:start + size], z_out.at[buf, chunk])
 
     def z_load(buf, slot):
         return pltpu.make_async_copy(z_hbm.at[slot], z_ref.at[buf], z_back.at[buf])
 
-    for chunk, (start, size) in enumerate(fwd_chunks):
+    for chunk, (start, size) in enumerate(row_chunks):
         pltpu.make_async_copy(dw_ref.at[start:start + size], z_hbm.at[2 * groups, start:start + size], z_out.at[1, chunk]).start()
     for load in loads:
         load.wait()
@@ -141,14 +141,15 @@
     def fwd_tile(buf, tid):
         run_max = jnp.full((8, tile), -jnp.inf, F32)
         run_sum = jnp.zeros((8, tile), F32)
-        for chunk, (start, size) in enumerate(fwd_chunks):
+        for chunk, (start, size) in enumerate(row_chunks):
             sl = slice(start, start + size)
             z_ref[buf, sl, :] = lax.dot_general(
                 w_ref[sl, :], h_all[tid], (((1,), (1,)), ((), ())), preferred_element_type=F32)
-            z_grp = z_ref[buf, sl, :].reshape(size // 8, 8, tile)
-            new_max = jnp.maximum(run_max, jnp.max(z_grp, axis=0))
-            run_sum = run_sum * jnp.exp(run_max - new_max) + jnp.sum(jnp.exp(z_grp - new_max[None]), axis=0)
-            run_max = new_max
+            for first, count in chunks(size, GROUP):
+                z_grp = z_ref[buf, start + first:start + first + count, :].reshape(count // 8, 8, tile)
+                new_max = jnp.maximum(run_max, jnp.max(z_grp, axis=0))
+                run_sum = run_sum * jnp.exp(run_max - new_max) + jnp.sum(jnp.exp(z_grp - new_max[None]), axis=0)
+                run_max = new_max
             z_store(buf, tid, chunk).start()
         tot_max = jnp.max(run_max, axis=0, keepdims=True)
         tot_sum = jnp.sum(run_sum * jnp.exp(run_max - tot_max), axis=0, keepdims=True)
@@ -197,11 +198,11 @@
 
         @pl.when(step > 0)
         def _():
-            for chunk in range(len(fwd_chunks)):
+            for chunk in range(len(row_chunks)):
                 z_store(0, 0, chunk).wait()
 
         fwd_tile(0, 2 * step)
-        for chunk in range(len(fwd_chunks)):
+        for chunk in range(len(row_chunks)):
             z_store(1, 0, chunk).wait()
         fwd_tile(1, 2 * step + 1)
         return carry
@@ -209,7 +210,7 @@
     lax.fori_loop(0, groups, fwd_pair, 0)
 
     for buf in range(2):
-        for chunk in range(len(fwd_chunks)):
+        for chunk in range(len(row_chunks)):
             z_store(buf, 0, chunk).wait()
 
     def pair_tile(pair, flip):
@@ -256,36 +257,43 @@
 
     inv_tokens = 1.0 / tokens
     log_tokens = jnp.log(jnp.float32(tokens))
-    bwd_chunks = chunks(rows, BWD_CHUNK)
-
-    def bwd_tile(buf, slot, tid, with_dw):
+
+    def bwd_tile(buf, tid, dh_slot=None, with_dw=True, last=False):
         where = pieces(tid)
-
         stats = [stat_loc] + [stat_in.at[i] for i in range(len(PEERS))]
         maxes, sums = [
             [jnp.concatenate([ref[block, quarter, kind] for block, quarter in where], axis=1) for ref in stats] for kind in range(2)]
         tot_max = functools.reduce(jnp.maximum, maxes)
         tot_sum = sum(s * jnp.exp(m - tot_max) for m, s in zip(maxes, sums))
         lse = tot_max + jnp.log(tot_sum)
-        lse_acc[...] += lse
         shift = lse + log_tokens
         tgt = jnp.concatenate([t_all[block, quarter] for block, quarter in where], axis=1) - me * rows
-        zt_sum = zt_acc[...]
-        for idx, (start, size) in enumerate(bwd_chunks):
+        if dh_slot is not None:
+            lse_acc[...] += lse
+            zt_sum = zt_acc[...]
+        for idx, (start, size) in enumerate(row_chunks):
             sl = slice(start, start + size)
             z = z_ref[buf, sl, :]
             mask = (lax.broadcasted_iota(jnp.int32, (size, tile), 0) + start) == tgt
             prob = jnp.exp(z - shift)
-            dz_ref[buf, sl, :] = jnp.where(mask, prob - inv_tokens, prob).astype(BF16)
-            zt_sum += jnp.sum(jnp.where(mask, z, 0.0).reshape(size // 8, 8, tile), axis=0)
+            dz_ref[sl, :] = jnp.where(mask, prob - inv_tokens, prob).astype(BF16)
             if with_dw:
-                dw_ref[sl, :] += jnp.dot(dz_ref[buf, sl, :], h_all[tid], preferred_element_type=F32)
-            dh_part = lax.dot_general(dz_ref[buf, sl, :], w_ref[sl, :], (((0,), (0,)), ((), ())), preferred_element_type=F32)
-            if idx == 0:
-                pbuf[slot] = dh_part
-            else:
-                pbuf[slot] += dh_part
-        zt_acc[...] = zt_sum
+                dw_ref[sl, :] += jnp.dot(dz_ref[sl, :], h_all[tid], preferred_element_type=F32)
+            if last:
+                dw_out(idx).start()
+            if dh_slot is not None:
+                zt_sum += jnp.sum(jnp.where(mask, z, 0.0).reshape(size // 8, 8, tile), axis=0)
+                dh_part = lax.dot_general(dz_ref[sl, :], w_ref[sl, :], (((0,), (0,)), ((), ())), preferred_element_type=F32)
+                if idx == 0:
+                    pbuf[dh_slot] = dh_part
+                else:
+                    pbuf[dh_slot] += dh_part
+        if dh_slot is not None:
+            zt_acc[...] = zt_sum
+
+    def dw_out(idx):
+        start, size = row_chunks[idx]
+        return pltpu.make_async_copy(dw_ref.at[start:start + size], dw_hbm.at[start:start + size], out_sem.at[2 + idx])
 
     def finish_pair(pair):
         kind, j = PAIRS[pair]
@@ -305,6 +313,16 @@
             add_into(slot, part * quarter_toks, quarter_toks, sources)
             ici_copy(pair, part).start()
 
+    def run_pair(pair, odd, slot, with_dw):
+        z_next = lax.rem(pair + 1, len(PAIRS))
+        bwd_tile(0, pair_tile(pair, 1), odd, with_dw)
+        d2d_copy(odd).start()
+        z_load(0, pair_tile(z_next, 1)).start()
+        z_load(1, 0).wait()
+        bwd_tile(1, pair_tile(pair, 0), 2 + slot, with_dw)
+        z_load(1, pair_tile(z_next, 0)).start()
+        d2d_copy(odd).wait_recv()
+
     def bwd_pair(pair, carry):
         odd = lax.rem(pair, 2)
 
@@ -316,51 +334,32 @@
         def _():
             wait_ici_sends(pair - 4)
 
-        @pl.when(pair >= 1)
-        def _():
-            z_load(0, 0).wait()
-
-        bwd_tile(0, odd, pair_tile(pair, 1), True)
-        d2d_copy(odd).start()
-        z_load(0, pair_tile(pair + 1, 1)).start()
-        z_load(1, 0).wait()
-        bwd_tile(1, 2 + lax.rem(pair, 4), pair_tile(pair, 0), True)
-        z_load(1, pair_tile(pair + 1, 0)).start()
-        d2d_copy(odd).wait_recv()
-        for pair_s in range(len(PAIRS) - 1):
+        z_load(0, 0).wait()
+        run_pair(pair, odd, lax.rem(pair, 4), True)
+        for pair_s in range(1, last):
             @pl.when(pair == pair_s)
             def _():
                 finish_pair(pair_s)
         return carry
 
     last = len(PAIRS) - 1
-    lax.fori_loop(0, last, bwd_pair, 0)
-
-    outs = [pltpu.make_async_copy(dw_ref, dw_hbm, out_sem.at[2])]
-    outs += [pltpu.make_async_copy(h_all.at[tile_id("own", 1 - i, 1)], htail_hbm.at[i], out_sem.at[3 + i]) for i in range(2)]
-    for out in outs:
-        out.start()
-    d2d_copy(last % 2).wait_send()
-    wait_ici_sends(last - 4)
+    run_pair(jnp.int32(0), 0, 0, False)
+    finish_pair(0)
+    lax.fori_loop(1, last + 1, bwd_pair, 0)
+
+    zt_row[...] = jnp.sum(zt_acc[...], axis=0, keepdims=True)
+
+    def zt_copy(peer):
+        slot = seen_from(peer)
+        return pltpu.make_async_remote_copy(
+            src_ref=zt_row, dst_ref=zt_in.at[slot], send_sem=zt_send.at[slot], recv_sem=zt_recv.at[slot],
+            device_id={"fsdp": dev(*peer)}, device_id_type=MESH)
+
+    for peer in PEERS:
+        zt_copy(peer).start()
     for buf in range(2):
         z_load(buf, 0).wait()
-        bwd_tile(buf, (last % 2, 2 + last % 4)[buf], tile_id("own", 1 - buf, 1), False)
-        outs.append(pltpu.make_async_copy(dz_ref.at[buf], dz_hbm.at[buf], out_sem.at[5 + buf]))
-        outs[-1].start()
-        if buf == 0:
-            d2d_copy(last % 2).start()
-
-    zt_row[...] = jnp.sum(zt_acc[...], axis=0, keepdims=True)
-
-    def zt_copy(peer):
-        slot = seen_from(peer)
-        return pltpu.make_async_remote_copy(
-            src_ref=zt_row, dst_ref=zt_in.at[slot], send_sem=zt_send.at[slot], recv_sem=zt_recv.at[slot],
-            device_id={"fsdp": dev(*peer)}, device_id_type=MESH)
-
-    for peer in PEERS:
-        zt_copy(peer).start()
-    d2d_copy(last % 2).wait_recv()
+        bwd_tile(buf, tile_id("across", 1 - buf, 0), last=buf == 1)
     finish_pair(last)
     for peer in PEERS:
         zt_copy(peer).wait()
@@ -383,16 +382,25 @@
         wait_ici_sends(pair % 4)
     for j in range(2):
         pltpu.make_async_copy(pbuf.at[2 + (6 + j) % 4], dh_hbm.at[j], out_sem.at[j]).wait()
-    for out in outs:
-        out.wait()
-
-
-def tail_kernel(dw_ref, dz_ref, h_ref, dh_ref, dw_out, dh_out):
-    tot = dw_ref[...]
-    for i in range(2):
-        tot = tot + jnp.dot(dz_ref[i], h_ref[i], preferred_element_type=F32)
-    dw_out[...] = tot
-    dh_out[...] = dh_ref[...]
+    for idx in range(len(row_chunks)):
+        dw_out(idx).wait()
+
+
+def copy_kernel(dw_hbm, dh_hbm, dw_out, dh_out, dw_buf, dh_buf, in_sem, out_sem):
+    moves = []
+    for src, buf, dst in ((dw_hbm, dw_buf, dw_out), (dh_hbm, dh_buf, dh_out)):
+        for start, size in chunks(src.shape[0], COPY_ROWS):
+            sl = slice(start, start + size)
+            moves.append((
+                pltpu.make_async_copy(src.at[sl], buf.at[sl], in_sem.at[len(moves)]),
+                pltpu.make_async_copy(buf.at[sl], dst.at[sl], out_sem.at[len(moves)])))
+    for load, _ in moves:
+        load.start()
+    for load, store in moves:
+        load.wait()
+        store.start()
+    for _, store in moves:
+        store.wait()
 
 
 def solution(mesh):
@@ -408,19 +416,18 @@
         any_spec = pl.BlockSpec(memory_space=pl.ANY)
         vmem, dma = pltpu.VMEM, pltpu.SemaphoreType.DMA
         shape = jax.ShapeDtypeStruct
-        loss_row, grad_h, dw_part, dz_tail, h_tail, _ = pl.pallas_call(
+        loss_row, grad_h, grad_w, _ = pl.pallas_call(
             functools.partial(head_kernel, groups, tokens),
             in_specs=[any_spec] * 3,
-            out_specs=[pl.BlockSpec(memory_space=pltpu.VMEM)] + [any_spec] * 5,
+            out_specs=[pl.BlockSpec(memory_space=pltpu.VMEM)] + [any_spec] * 3,
             out_shape=[
-                shape((1, 128), F32), shape((2, tile, width), F32), shape((rows, width), F32), shape((2, rows, tile), BF16),
-                shape((2, tile, width), BF16), shape((2 * groups + 1, rows, tile), F32)],
+                shape((1, 128), F32), shape((2, tile, width), F32), shape((rows, width), F32), shape((2 * groups + 1, rows, tile), F32)],
             scratch_shapes=[
                 vmem((2 * groups, tile, width), BF16),
                 vmem((groups, 4, 1, quarter), jnp.int32),
                 vmem((rows, width), BF16),
                 vmem((2, rows, tile), F32),
-                vmem((2, rows, tile), BF16),
+                vmem((rows, tile), BF16),
                 vmem((rows, width), F32),
                 vmem((6, tile, width), F32),
                 vmem((2, tile, width), F32),
@@ -433,24 +440,21 @@
                 vmem((1, tile), F32),
                 vmem((peers, 1, tile), F32),
                 dma((4,)), dma((4 * peers,)), dma((4 * peers,)), dma((peers,)), dma((peers,)), dma, dma,
-                dma((2,)), dma((2,)), dma((8,)), dma((4,)), dma((8,)), dma((peers,)), dma((peers,)), dma((7,)),
-                dma((2, len(chunks(rows, FWD_CHUNK)))), dma((2,)),
+                dma((2,)), dma((2,)), dma((8,)), dma((4,)), dma((8,)), dma((peers,)), dma((peers,)), dma((2 + len(chunks(rows, CHUNK)),)),
+                dma((2, len(chunks(rows, CHUNK)))), dma((2,)),
             ],
             compiler_params=pltpu.CompilerParams(collective_id=0, has_side_effects=True, vmem_limit_bytes=67_000_000),
             name="head",
         )(hidden.reshape(2, tile, width), targets.reshape(4, 1, quarter), weight)
-        steps = pl.cdiv(rows, TAIL_ROWS)
-        row_spec = pl.BlockSpec((TAIL_ROWS, width), lambda i: (i, 0))
-        dh_spec = pl.BlockSpec((tok_loc // steps, width), lambda i: (i, 0))
+        copies = len(chunks(rows, COPY_ROWS)) + len(chunks(tok_loc, COPY_ROWS))
         grad_w, grad_h = pl.pallas_call(
-            tail_kernel,
-            grid=(steps,),
-            in_specs=[row_spec, pl.BlockSpec((2, TAIL_ROWS, tile), lambda i: (0, i, 0)),
-                      pl.BlockSpec((2, tile, width), lambda i: (0, 0, 0)), dh_spec],
-            out_specs=[row_spec, dh_spec],
+            copy_kernel,
+            in_specs=[any_spec] * 2,
+            out_specs=[any_spec] * 2,
             out_shape=[shape((rows, width), F32), shape((tok_loc, width), F32)],
-            name="tail",
-        )(dw_part, dz_tail, h_tail, grad_h.reshape(tok_loc, width))
+            scratch_shapes=[vmem((rows, width), F32), vmem((tok_loc, width), F32), dma((copies,)), dma((copies,))],
+            name="results",
+        )(grad_w, grad_h.reshape(tok_loc, width))
         return loss_row[0, :1], grad_h, grad_w
 
     return jax.shard_map(local_head, mesh=mesh, in_specs=(tok_spec, P(("dp", "fsdp")), P("fsdp", None)), out_specs=(P("dp"), tok_spec, tok_spec), check_vma=False)

time: 169 us -> 162 us (0.959)
  Pallas kernels: 167 us -> 160 us
    pallas_call x1, Pallas kernels: 14.3 us -> 8.03 us  [local_head(): pl.pallas_call(copy_kernel, in_specs=[any_spec] * 2, out_specs=[any_spec]...]
where the time goes in v5:
time: 162 us
  Pallas kernels  160 us (99%)
  between operations  1.82 us (1%)
    pallas_call x1, Pallas kernels, local_head(): pl.pallas_call(functools.partial(head_kernel, groups, tokens), in_specs=[...  152 us
    pallas_call x1, Pallas kernels, local_head(): pl.pallas_call(copy_kernel, in_specs=[any_spec] * 2, out_specs=[any_spec]...  8.03 us

profile of v5, /device:TPU:113, one launch (start us, length us, event | category | flops | bytes accessed | tf_op | source)
XLA Modules:
  0.0 162.2 jit_solution(9603340235695941174)
XLA Ops:
  0.6 152.4 %head.1 = (f32[1,128]{1,0:T(1,128)}, f32[2,512,512]{2,1,0:T(8,128)}, f32[4016,512]{1,0:T(8,128)}, f32[17,4016,512]{2,1,0:T(8,128)}) custom-call(bf16[2,512,512]{2,1,0:T(8,128)(2,1)} %bitcast.6, s32[4,1,256]{2,1,0:T(1,128)} %bitcast.7, bf16[4016,512]{1,0:T(8,128)(2,1)} %w_hbm.1), custom_call_target="tpu_custom_call" | custom-call | tf_op jit(solution)/shard_map/head/pallas_call | solution.py:419
  153.0 0.0 copy-start
  153.0 8.0 %results.1 = (f32[4016,512]{1,0:T(8,128)}, f32[1024,512]{1,0:T(8,128)}) custom-call(f32[4016,512]{1,0:T(8,128)} %get-tuple-element.9.dw_hbm, f32[1024,512]{1,0:T(8,128)} %bitcast.5), custom_call_target="tpu_custom_call" | custom-call | tf_op jit(solution)/shard_map/results/pallas_call | solution.py:450
  161.1 0.0 copy-done
Async XLA Ops:
  153.0 8.0 %copy-start = (f32[1,128]{1,0:T(1,128)S(1)}, f32[1,128]{1,0:T(1,128)}, u32[]{:S(2)}) copy-start(f32[1,128]{1,0:T(1,128)} %get-tuple-element.8) | copy-start | bytes 1540

commit v6 on v5

--- a/solution.py
+++ b/solution.py
@@ -21,16 +21,18 @@
 PEER_SLOT = {peer: slot for slot, peer in enumerate(PEERS)}
 
 def tile_id(kind, flip, j):
-    if kind == "mixed":
-        return 4 + 2 * flip + 4 * (j // 2) + j % 2
-    return {"own": 0, "across": 12}[kind] + 2 * flip + j
+    if kind == "own":
+        return 2 * flip + j
+    return {"mixed": 4, "across": 12}[kind] + 2 * j + flip
 
 
 def place(owner, quarter):
     dx, flip = owner
     if dx in (LEFT, RIGHT):
         return tile_id("mixed", flip, quarter), 0 if dx == RIGHT else 1
-    return tile_id("own" if dx == 0 else "across", flip, quarter // 2), quarter % 2
+    if dx == ACROSS:
+        return tile_id("across", flip, quarter % 2), quarter // 2
+    return tile_id("own", flip, quarter // 2), quarter % 2
 
 
 PAIRS = [("across", 0), ("across", 1)] + [("mixed", j) for j in range(4)] + [("own", 0), ("own", 1)]
@@ -122,20 +124,22 @@
     load_w.wait()
 
     def pieces(tid):
-        grp = lax.div(tid, 4)
-        flip = lax.rem(lax.div(tid, 2), 2)
-        j = lax.rem(tid, 2)
-        mixed = lax.rem(lax.div(grp + 1, 2), 2)
+        step, sub = lax.div(tid, 2), lax.rem(tid, 2)
+        is_own = 1 - lax.div(lax.div(step, 2) + 3, 4)
+        is_across = lax.div(step, 6)
+        mixed = 1 - is_own - is_across
+        flip = is_own * step + (1 - is_own) * sub
+        j = is_own * sub + (1 - is_own) * (step - 2 - 4 * is_across)
         out = []
         for part in range(2):
-            dx = mixed * (RIGHT, LEFT)[part] + lax.div(grp, 3) * ACROSS
-            quarter = mixed * (2 * lax.div(grp, 2) + j) + (1 - mixed) * (2 * j + part)
+            dx = mixed * (RIGHT, LEFT)[part] + is_across * ACROSS
+            quarter = mixed * j + is_own * (2 * j + part) + is_across * (j + 2 * part)
             out.append((dev(dx, flip), quarter))
         return out
 
-    def stat_copy(peer, block, quarter):
-        return pltpu.make_async_remote_copy(
-            src_ref=stat_loc.at[block, quarter], dst_ref=stat_in.at[seen_from(peer), block, quarter],
+    def stat_copy(peer, block):
+        return pltpu.make_async_remote_copy(
+            src_ref=stat_loc.at[block], dst_ref=stat_in.at[seen_from(peer), block],
             send_sem=stat_send, recv_sem=stat_recv, device_id={"fsdp": dev(*peer)}, device_id_type=MESH)
 
     def fwd_tile(buf, tid):
@@ -157,9 +161,6 @@
             lanes = slice(part * quarter_toks, (part + 1) * quarter_toks)
             stat_loc[block, quarter, 0] = tot_max[:, lanes]
             stat_loc[block, quarter, 1] = tot_sum[:, lanes]
-        for block, quarter in pieces(tid):
-            for peer in PEERS:
-                stat_copy(peer, block, quarter).start()
 
     def fwd_pair(step, carry):
         @pl.when(step == 1)
@@ -167,34 +168,28 @@
             for quarter in range(4):
                 gather_recv(PARTNER, quarter)
 
-        for late in range(2):
-            @pl.when(step == 2 + 2 * late)
+        for j in range(4):
+            @pl.when(step == 2 + j)
             def _():
-                for quarter in (2 * late, 2 * late + 1):
-                    for owner in (left, right):
-                        gather_recv(owner, quarter)
-                        if late == 0 and owner == left:
-                            gather_copy(left, quarter, right).start()
-                        if late == 1 and owner == right:
-                            gather_copy(right, quarter, left).start()
-                        gather_copy(owner, quarter, PARTNER).start()
-
-            @pl.when(step == 3 + 2 * late)
+                gather_recv(left, j)
+                gather_recv(right, j)
+                if j < 2:
+                    gather_copy(left, j, right).start()
+                else:
+                    gather_copy(right, j, left).start()
+                gather_copy(left, j, PARTNER).start()
+                gather_copy(right, j, PARTNER).start()
+
+        for j in range(2):
+            @pl.when(step == 6 + j)
             def _():
-                for quarter in (2 * late, 2 * late + 1):
-                    gather_recv((LEFT, 1), quarter)
-                    gather_recv((RIGHT, 1), quarter)
-
-        @pl.when(step == 6)
-        def _():
-            for quarter in range(4):
-                gather_recv(across, quarter)
-                gather_copy(across, quarter, PARTNER).start()
-
-        @pl.when(step == 7)
-        def _():
-            for quarter in range(4):
-                gather_recv((ACROSS, 1), quarter)
+                if j == 0:
+                    for owner in [OWN] + PEERS[:5]:
+                        for peer in PEERS:
+                            stat_copy(peer, dev(*owner)).start()
+                for quarter in (j, j + 2):
+                    gather_recv(across, quarter)
+                    gather_copy(across, quarter, PARTNER).start()
 
         @pl.when(step > 0)
         def _():
@@ -202,6 +197,18 @@
                 z_store(0, 0, chunk).wait()
 
         fwd_tile(0, 2 * step)
+        for j in range(4):
+            @pl.when(step == 2 + j)
+            def _():
+                gather_recv((LEFT, 1), j)
+                gather_recv((RIGHT, 1), j)
+
+        for j in range(2):
+            @pl.when(step == 6 + j)
+            def _():
+                gather_recv((ACROSS, 1), j)
+                gather_recv((ACROSS, 1), j + 2)
+
         for chunk in range(len(row_chunks)):
             z_store(1, 0, chunk).wait()
         fwd_tile(1, 2 * step + 1)
@@ -209,14 +216,17 @@
 
     lax.fori_loop(0, groups, fwd_pair, 0)
 
+    for owner in PEERS[5:]:
+        for peer in PEERS:
+            stat_copy(peer, dev(*owner)).start()
+
+    def pair_tile(pair, flip):
+        return lax.rem(lax.shift_right_logical(jnp.int32(PAIR_CODE), 4 * pair), 16) + flip * (1 + lax.div(pair, 6))
+
     for buf in range(2):
         for chunk in range(len(row_chunks)):
             z_store(buf, 0, chunk).wait()
-
-    def pair_tile(pair, flip):
-        return lax.rem(lax.shift_right_logical(jnp.int32(PAIR_CODE), 4 * pair), 16) + 2 * flip
-
-    z_load(1, pair_tile(0, 0)).start()
+        z_load(buf, tile_id("across", 1 - buf, 0)).start()
     for peer in PEERS:
         target_copy(peer).wait_recv()
     all_stats = pltpu.make_async_remote_copy(
@@ -307,9 +317,9 @@
             return
         for part in range(2):
             sources = [d2d_in.at[pair % 2, parts[part]]]
-            if kind == "mixed" and j % 2 == part:
-                ici_copy(j // 2, part).wait_recv()
-                sources.append(ring_in.at[part, j // 2])
+            if kind == "mixed" and j // 2 == part:
+                ici_copy(j % 2, part).wait_recv()
+                sources.append(ring_in.at[part, j % 2])
             add_into(slot, part * quarter_toks, quarter_toks, sources)
             ici_copy(pair, part).start()
 
@@ -343,6 +353,7 @@
         return carry
 
     last = len(PAIRS) - 1
+    z_load(0, 0).wait()
     run_pair(jnp.int32(0), 0, 0, False)
     finish_pair(0)
     lax.fori_loop(1, last + 1, bwd_pair, 0)

time: 162 us -> 158 us (0.975)
  Pallas kernels: 160 us -> 156 us
    pallas_call x1, Pallas kernels: 152 us -> 148 us  [local_head(): pl.pallas_call(functools.partial(head_kernel, groups, tokens), in_specs=[...]
where the time goes in v6:
time: 158 us
  Pallas kernels  156 us (99%)
  between operations  1.82 us (1%)
    pallas_call x1, Pallas kernels, local_head(): pl.pallas_call(functools.partial(head_kernel, groups, tokens), in_specs=[...  148 us
    pallas_call x1, Pallas kernels, local_head(): pl.pallas_call(copy_kernel, in_specs=[any_spec] * 2, out_specs=[any_spec]...  8.03 us

profile of v6, /device:TPU:113, one launch (start us, length us, event | category | flops | bytes accessed | tf_op | source)
XLA Modules:
  0.0 158.0 jit_solution(18008204938349827997)
XLA Ops:
  0.6 148.1 %head.1 = (f32[1,128]{1,0:T(1,128)}, f32[2,512,512]{2,1,0:T(8,128)}, f32[4016,512]{1,0:T(8,128)}, f32[17,4016,512]{2,1,0:T(8,128)}) custom-call(bf16[2,512,512]{2,1,0:T(8,128)(2,1)} %bitcast.6, s32[4,1,256]{2,1,0:T(1,128)} %bitcast.7, bf16[4016,512]{1,0:T(8,128)(2,1)} %w_hbm.1), custom_call_target="tpu_custom_call" | custom-call | tf_op jit(solution)/shard_map/head/pallas_call | solution.py:430
  148.8 0.0 copy-start
  148.8 8.0 %results.1 = (f32[4016,512]{1,0:T(8,128)}, f32[1024,512]{1,0:T(8,128)}) custom-call(f32[4016,512]{1,0:T(8,128)} %get-tuple-element.9.dw_hbm, f32[1024,512]{1,0:T(8,128)} %bitcast.5), custom_call_target="tpu_custom_call" | custom-call | tf_op jit(solution)/shard_map/results/pallas_call | solution.py:461
  156.8 0.0 copy-done
Async XLA Ops:
  148.8 8.0 %copy-start = (f32[1,128]{1,0:T(1,128)S(1)}, f32[1,128]{1,0:T(1,128)}, u32[]{:S(2)}) copy-start(f32[1,128]{1,0:T(1,128)} %get-tuple-element.8) | copy-start | bytes 1540

commit v7 on v6

--- a/solution.py
+++ b/solution.py
@@ -13,7 +13,8 @@
 CORES = 2
 CHUNK = 1008
 GROUP = 112
-COPY_ROWS = 512
+SUMS = 3
+VMEM_LIMIT = 56_000_000
 
 LEFT, RIGHT, ACROSS = 3, 1, 2
 OWN, PARTNER = (0, 0), (0, 1)
@@ -43,11 +44,11 @@
     return [(start, min(step, rows - start)) for start in range(0, rows, step)]
 
 
-def head_kernel(groups, tokens, hid_hbm, tgt_hbm, w_hbm, loss_ref, dh_hbm, dw_hbm, z_hbm,
-                h_all, t_all, w_ref, z_ref, dz_ref, dw_ref, pbuf, d2d_in, ring_in, fin_in,
+def head_kernel(groups, tokens, hid_hbm, tgt_hbm, w_hbm, loss_ref, dh_ref, dw_ref, z_hbm,
+                h_all, t_all, w_ref, z_ref, dz_ref, pbuf, d2d_in, ring_in, fin_in,
                 stat_loc, stat_in, lse_acc, zt_acc, zt_row, zt_in,
                 load_sem, ag_send, ag_recv, tgt_send, tgt_recv, stat_send, stat_recv,
-                d2d_send, d2d_recv, ici_send, ring_recv, fin_recv, zt_send, zt_recv, out_sem, z_out, z_back):
+                d2d_send, d2d_recv, ici_send, ring_recv, fin_recv, zt_send, zt_recv, z_out, z_back):
     chips = groups // CORES
     me = lax.axis_index("fsdp")
     chip = lax.div(me, CORES)
@@ -245,7 +246,7 @@
         else:
             dst, recv = fin_in.at[part, j // 2, parts[j % 2]], fin_recv.at[part * 4 + j]
         return pltpu.make_async_remote_copy(
-            src_ref=pbuf.at[2 + pair % 4, parts[part]], dst_ref=dst, send_sem=ici_send.at[(pair % 4) * 2 + part], recv_sem=recv,
+            src_ref=pbuf.at[2 + pair % SUMS, parts[part]], dst_ref=dst, send_sem=ici_send.at[(pair % SUMS) * 2 + part], recv_sem=recv,
             device_id={"fsdp": dev(*(right, left)[part])}, device_id_type=MESH)
 
     def wait_ici_sends(slot):
@@ -254,21 +255,24 @@
                 src_ref=pbuf.at[2 + slot, parts[part]], dst_ref=ring_in.at[0, 0], send_sem=ici_send.at[slot * 2 + part],
                 recv_sem=ring_recv.at[0], device_id={"fsdp": me}, device_id_type=MESH).wait_send()
 
-    def add_into(slot, base, count, sources):
+    def add_into(slot, base, count, sources, dst=None):
         def body(i, carry):
             off = pl.multiple_of(i * 64, 64)
             sl = pl.ds(base + off, 64)
             tot = pbuf[slot, sl, :]
             for src in sources:
                 tot = tot + src[pl.ds(off, 64), :]
-            pbuf[slot, sl, :] = tot
+            if dst is None:
+                pbuf[slot, sl, :] = tot
+            else:
+                dst[sl, :] = tot
             return carry
         lax.fori_loop(0, count // 64, body, 0)
 
     inv_tokens = 1.0 / tokens
     log_tokens = jnp.log(jnp.float32(tokens))
 
-    def bwd_tile(buf, tid, dh_slot=None, with_dw=True, last=False):
+    def bwd_tile(buf, tid, dh_slot=None, with_dw=True):
         where = pieces(tid)
         stats = [stat_loc] + [stat_in.at[i] for i in range(len(PEERS))]
         maxes, sums = [
@@ -286,14 +290,12 @@
             z = z_ref[buf, sl, :]
             mask = (lax.broadcasted_iota(jnp.int32, (size, tile), 0) + start) == tgt
             prob = jnp.exp(z - shift)
-            dz_ref[sl, :] = jnp.where(mask, prob - inv_tokens, prob).astype(BF16)
+            dz_ref[idx % 2, :size, :] = jnp.where(mask, prob - inv_tokens, prob).astype(BF16)
             if with_dw:
-                dw_ref[sl, :] += jnp.dot(dz_ref[sl, :], h_all[tid], preferred_element_type=F32)
-            if last:
-                dw_out(idx).start()
+                dw_ref[sl, :] += jnp.dot(dz_ref[idx % 2, :size, :], h_all[tid], preferred_element_type=F32)
             if dh_slot is not None:
                 zt_sum += jnp.sum(jnp.where(mask, z, 0.0).reshape(size // 8, 8, tile), axis=0)
-                dh_part = lax.dot_general(dz_ref[sl, :], w_ref[sl, :], (((0,), (0,)), ((), ())), preferred_element_type=F32)
+                dh_part = lax.dot_general(dz_ref[idx % 2, :size, :], w_ref[sl, :], (((0,), (0,)), ((), ())), preferred_element_type=F32)
                 if idx == 0:
                     pbuf[dh_slot] = dh_part
                 else:
@@ -301,19 +303,14 @@
         if dh_slot is not None:
             zt_acc[...] = zt_sum
 
-    def dw_out(idx):
-        start, size = row_chunks[idx]
-        return pltpu.make_async_copy(dw_ref.at[start:start + size], dw_hbm.at[start:start + size], out_sem.at[2 + idx])
-
     def finish_pair(pair):
         kind, j = PAIRS[pair]
-        slot = 2 + pair % 4
+        slot = 2 + pair % SUMS
         if kind == "own":
             for part in range(2):
                 for q in range(2):
                     ici_copy(2 + 2 * j + q, part).wait_recv()
-            add_into(slot, 0, tile, [d2d_in.at[pair % 2], fin_in.at[0, j], fin_in.at[1, j]])
-            pltpu.make_async_copy(pbuf.at[slot], dh_hbm.at[j], out_sem.at[j]).start()
+            add_into(slot, 0, tile, [d2d_in.at[pair % 2], fin_in.at[0, j], fin_in.at[1, j]], dh_ref.at[j])
             return
         for part in range(2):
             sources = [d2d_in.at[pair % 2, parts[part]]]
@@ -340,12 +337,12 @@
         def _():
             d2d_copy(odd).wait_send()
 
-        @pl.when(pair >= 4)
+        @pl.when(pair >= SUMS)
         def _():
-            wait_ici_sends(pair - 4)
+            wait_ici_sends(lax.rem(pair, SUMS))
 
         z_load(0, 0).wait()
-        run_pair(pair, odd, lax.rem(pair, 4), True)
+        run_pair(pair, odd, lax.rem(pair, SUMS), True)
         for pair_s in range(1, last):
             @pl.when(pair == pair_s)
             def _():
@@ -370,7 +367,7 @@
         zt_copy(peer).start()
     for buf in range(2):
         z_load(buf, 0).wait()
-        bwd_tile(buf, tile_id("across", 1 - buf, 0), last=buf == 1)
+        bwd_tile(buf, tile_id("across", 1 - buf, 0))
     finish_pair(last)
     for peer in PEERS:
         zt_copy(peer).wait()
@@ -389,29 +386,8 @@
     all_stats.wait_send()
     for slot in range(2):
         d2d_copy(slot).wait_send()
-    for pair in (4, 5):
-        wait_ici_sends(pair % 4)
-    for j in range(2):
-        pltpu.make_async_copy(pbuf.at[2 + (6 + j) % 4], dh_hbm.at[j], out_sem.at[j]).wait()
-    for idx in range(len(row_chunks)):
-        dw_out(idx).wait()
-
-
-def copy_kernel(dw_hbm, dh_hbm, dw_out, dh_out, dw_buf, dh_buf, in_sem, out_sem):
-    moves = []
-    for src, buf, dst in ((dw_hbm, dw_buf, dw_out), (dh_hbm, dh_buf, dh_out)):
-        for start, size in chunks(src.shape[0], COPY_ROWS):
-            sl = slice(start, start + size)
-            moves.append((
-                pltpu.make_async_copy(src.at[sl], buf.at[sl], in_sem.at[len(moves)]),
-                pltpu.make_async_copy(buf.at[sl], dst.at[sl], out_sem.at[len(moves)])))
-    for load, _ in moves:
-        load.start()
-    for load, store in moves:
-        load.wait()
-        store.start()
-    for _, store in moves:
-        store.wait()
+    for pair in range(8 - SUMS, 6):
+        wait_ici_sends(pair % SUMS)
 
 
 def solution(mesh):
@@ -430,17 +406,16 @@
         loss_row, grad_h, grad_w, _ = pl.pallas_call(
             functools.partial(head_kernel, groups, tokens),
             in_specs=[any_spec] * 3,
-            out_specs=[pl.BlockSpec(memory_space=pltpu.VMEM)] + [any_spec] * 3,
+            out_specs=[pl.BlockSpec(memory_space=pltpu.VMEM)] * 3 + [any_spec],
             out_shape=[
-                shape((1, 128), F32), shape((2, tile, width), F32), shape((rows, width), F32), shape((2 * groups + 1, rows, tile), F32)],
+                shape((1, 128), F32), vmem((2, tile, width), F32), vmem((rows, width), F32), shape((2 * groups + 1, rows, tile), F32)],
             scratch_shapes=[
                 vmem((2 * groups, tile, width), BF16),
                 vmem((groups, 4, 1, quarter), jnp.int32),
                 vmem((rows, width), BF16),
                 vmem((2, rows, tile), F32),
-                vmem((rows, tile), BF16),
-                vmem((rows, width), F32),
-                vmem((6, tile, width), F32),
+                vmem((2, CHUNK, tile), BF16),
+                vmem((2 + SUMS, tile, width), F32),
                 vmem((2, tile, width), F32),
                 vmem((2, 2, quarter, width), F32),
                 vmem((2, 2, tile, width), F32),
@@ -451,21 +426,12 @@
                 vmem((1, tile), F32),
                 vmem((peers, 1, tile), F32),
                 dma((4,)), dma((4 * peers,)), dma((4 * peers,)), dma((peers,)), dma((peers,)), dma, dma,
-                dma((2,)), dma((2,)), dma((8,)), dma((4,)), dma((8,)), dma((peers,)), dma((peers,)), dma((2 + len(chunks(rows, CHUNK)),)),
+                dma((2,)), dma((2,)), dma((2 * SUMS,)), dma((4,)), dma((8,)), dma((peers,)), dma((peers,)),
                 dma((2, len(chunks(rows, CHUNK)))), dma((2,)),
             ],
-            compiler_params=pltpu.CompilerParams(collective_id=0, has_side_effects=True, vmem_limit_bytes=67_000_000),
+            compiler_params=pltpu.CompilerParams(collective_id=0, has_side_effects=True, vmem_limit_bytes=VMEM_LIMIT),
             name="head",
         )(hidden.reshape(2, tile, width), targets.reshape(4, 1, quarter), weight)
-        copies = len(chunks(rows, COPY_ROWS)) + len(chunks(tok_loc, COPY_ROWS))
-        grad_w, grad_h = pl.pallas_call(
-            copy_kernel,
-            in_specs=[any_spec] * 2,
-            out_specs=[any_spec] * 2,
-            out_shape=[shape((rows, width), F32), shape((tok_loc, width), F32)],
-            scratch_shapes=[vmem((rows, width), F32), vmem((tok_loc, width), F32), dma((copies,)), dma((copies,))],
-            name="results",
-        )(grad_w, grad_h.reshape(tok_loc, width))
-        return loss_row[0, :1], grad_h, grad_w
+        return loss_row[0, :1], grad_h.reshape(tok_loc, width), grad_w
 
     return jax.shard_map(local_head, mesh=mesh, in_specs=(tok_spec, P(("dp", "fsdp")), P("fsdp", None)), out_specs=(P("dp"), tok_spec, tok_spec), check_vma=False)

time: 158 us -> 162 us (1.025)
  local copies, waits for them, and re-layouts: 0.01 us -> 4.66 us
    pallas_call x1 -> x0, Pallas kernels: 8.03 us -> none  [local_head(): pl.pallas_call(copy_kernel, in_specs=[any_spec] * 2, out_specs=[any_spec]...]
    pallas_call x1, Pallas kernels: 148 us -> 155 us  [local_head(): pl.pallas_call(functools.partial(head_kernel, groups, tokens), in_specs=[...]
    unnamed x2 -> x4, local copies, waits for them, and re-layouts: 0.01 us -> 4.66 us
where the time goes in v7:
time: 162 us; the launch traced here: 161 us
  Pallas kernels  155 us (96%)
  local copies, waits for them, and re-layouts  4.66 us (3%)
  between operations  1.81 us (1%)
    pallas_call x1, Pallas kernels, local_head(): pl.pallas_call(functools.partial(head_kernel, groups, tokens), in_specs=[...  155 us
    unnamed x4, local copies, waits for them, and re-layouts  4.66 us

profile of v7, /device:TPU:113, one launch (start us, length us, event | category | flops | bytes accessed | tf_op | source)
XLA Modules:
  0.0 161.4 jit_solution(12038316245256514557)
XLA Ops:
  0.6 155.0 %head.1 = (f32[1,128]{1,0:T(1,128)}, f32[2,512,512]{2,1,0:T(8,128)S(1)}, f32[4016,512]{1,0:T(8,128)S(1)}, f32[17,4016,512]{2,1,0:T(8,128)}) custom-call(bf16[2,512,512]{2,1,0:T(8,128)(2,1)} %bitcast.6, s32[4,1,256]{2,1,0:T(1,128)} %bitcast.7, bf16[4016,512]{1,0:T(8,128)(2,1)} %w_hbm.1), custom_call_target="tpu_custom_call" | custom-call | tf_op jit(solution)/shard_map/head/pallas_call | solution.py:406
  155.6 1.3 copy.9
  156.9 0.0 copy-start
  156.9 3.3 %copy.10 = f32[4016,512]{1,0:T(8,128)} copy(f32[4016,512]{1,0:T(8,128)S(1)} %get-tuple-element.11) | data formatting | bytes 16449536
  160.3 0.0 copy-done
Async XLA Ops:
  156.9 3.3 %copy-start = (f32[1,128]{1,0:T(1,128)S(1)}, f32[1,128]{1,0:T(1,128)}, u32[]{:S(2)}) copy-start(f32[1,128]{1,0:T(1,128)} %get-tuple-element.6) | copy-start | bytes 1540

commit v8 on v7

--- a/solution.py
+++ b/solution.py
@@ -14,7 +14,7 @@
 CHUNK = 1008
 GROUP = 112
 SUMS = 3
-VMEM_LIMIT = 56_000_000
+VMEM_LIMIT = 53_000_000
 
 LEFT, RIGHT, ACROSS = 3, 1, 2
 OWN, PARTNER = (0, 0), (0, 1)
@@ -44,8 +44,8 @@
     return [(start, min(step, rows - start)) for start in range(0, rows, step)]
 
 
-def head_kernel(groups, tokens, hid_hbm, tgt_hbm, w_hbm, loss_ref, dh_ref, dw_ref, z_hbm,
-                h_all, t_all, w_ref, z_ref, dz_ref, pbuf, d2d_in, ring_in, fin_in,
+def head_kernel(groups, tokens, hid_hbm, tgt_hbm, w_hbm, loss_ref, pbuf, dw_ref, z_hbm,
+                h_all, t_all, w_ref, z_ref, dz_ref, d2d_in, ring_in, fin_in,
                 stat_loc, stat_in, lse_acc, zt_acc, zt_row, zt_in,
                 load_sem, ag_send, ag_recv, tgt_send, tgt_recv, stat_send, stat_recv,
                 d2d_send, d2d_recv, ici_send, ring_recv, fin_recv, zt_send, zt_recv, z_out, z_back):
@@ -255,17 +255,14 @@
                 src_ref=pbuf.at[2 + slot, parts[part]], dst_ref=ring_in.at[0, 0], send_sem=ici_send.at[slot * 2 + part],
                 recv_sem=ring_recv.at[0], device_id={"fsdp": me}, device_id_type=MESH).wait_send()
 
-    def add_into(slot, base, count, sources, dst=None):
+    def add_into(slot, base, count, sources):
         def body(i, carry):
             off = pl.multiple_of(i * 64, 64)
             sl = pl.ds(base + off, 64)
             tot = pbuf[slot, sl, :]
             for src in sources:
                 tot = tot + src[pl.ds(off, 64), :]
-            if dst is None:
-                pbuf[slot, sl, :] = tot
-            else:
-                dst[sl, :] = tot
+            pbuf[slot, sl, :] = tot
             return carry
         lax.fori_loop(0, count // 64, body, 0)
 
@@ -290,12 +287,12 @@
             z = z_ref[buf, sl, :]
             mask = (lax.broadcasted_iota(jnp.int32, (size, tile), 0) + start) == tgt
             prob = jnp.exp(z - shift)
-            dz_ref[idx % 2, :size, :] = jnp.where(mask, prob - inv_tokens, prob).astype(BF16)
+            dz_ref[sl, :] = jnp.where(mask, prob - inv_tokens, prob).astype(BF16)
             if with_dw:
-                dw_ref[sl, :] += jnp.dot(dz_ref[idx % 2, :size, :], h_all[tid], preferred_element_type=F32)
+                dw_ref[sl, :] += jnp.dot(dz_ref[sl, :], h_all[tid], preferred_element_type=F32)
             if dh_slot is not None:
                 zt_sum += jnp.sum(jnp.where(mask, z, 0.0).reshape(size // 8, 8, tile), axis=0)
-                dh_part = lax.dot_general(dz_ref[idx % 2, :size, :], w_ref[sl, :], (((0,), (0,)), ((), ())), preferred_element_type=F32)
+                dh_part = lax.dot_general(dz_ref[sl, :], w_ref[sl, :], (((0,), (0,)), ((), ())), preferred_element_type=F32)
                 if idx == 0:
                     pbuf[dh_slot] = dh_part
                 else:
@@ -310,7 +307,7 @@
             for part in range(2):
                 for q in range(2):
                     ici_copy(2 + 2 * j + q, part).wait_recv()
-            add_into(slot, 0, tile, [d2d_in.at[pair % 2], fin_in.at[0, j], fin_in.at[1, j]], dh_ref.at[j])
+            add_into(slot, 0, tile, [d2d_in.at[pair % 2], fin_in.at[0, j], fin_in.at[1, j]])
             return
         for part in range(2):
             sources = [d2d_in.at[pair % 2, parts[part]]]
@@ -403,19 +400,18 @@
         any_spec = pl.BlockSpec(memory_space=pl.ANY)
         vmem, dma = pltpu.VMEM, pltpu.SemaphoreType.DMA
         shape = jax.ShapeDtypeStruct
-        loss_row, grad_h, grad_w, _ = pl.pallas_call(
+        loss_row, sums, grad_w, _ = pl.pallas_call(
             functools.partial(head_kernel, groups, tokens),
             in_specs=[any_spec] * 3,
             out_specs=[pl.BlockSpec(memory_space=pltpu.VMEM)] * 3 + [any_spec],
             out_shape=[
-                shape((1, 128), F32), vmem((2, tile, width), F32), vmem((rows, width), F32), shape((2 * groups + 1, rows, tile), F32)],
+                shape((1, 128), F32), vmem((2 + SUMS, tile, width), F32), vmem((rows, width), F32), shape((2 * groups + 1, rows, tile), F32)],
             scratch_shapes=[
                 vmem((2 * groups, tile, width), BF16),
                 vmem((groups, 4, 1, quarter), jnp.int32),
                 vmem((rows, width), BF16),
                 vmem((2, rows, tile), F32),
-                vmem((2, CHUNK, tile), BF16),
-                vmem((2 + SUMS, tile, width), F32),
+                vmem((rows, tile), BF16),
                 vmem((2, tile, width), F32),
                 vmem((2, 2, quarter, width), F32),
                 vmem((2, 2, tile, width), F32),
@@ -432,6 +428,7 @@
             compiler_params=pltpu.CompilerParams(collective_id=0, has_side_effects=True, vmem_limit_bytes=VMEM_LIMIT),
             name="head",
         )(hidden.reshape(2, tile, width), targets.reshape(4, 1, quarter), weight)
-        return loss_row[0, :1], grad_h.reshape(tok_loc, width), grad_w
+        first = 2 + (len(PAIRS) - 2) % SUMS
+        return loss_row[0, :1], sums[first:first + 2].reshape(tok_loc, width), grad_w
 
     return jax.shard_map(local_head, mesh=mesh, in_specs=(tok_spec, P(("dp", "fsdp")), P("fsdp", None)), out_specs=(P("dp"), tok_spec, tok_spec), check_vma=False)

time: 162 us -> 153 us (0.944)
  Pallas kernels: 155 us -> 146 us
    pallas_call x1, Pallas kernels: 155 us -> 146 us  [local_head(): pl.pallas_call(functools.partial(head_kernel, groups, tokens), in_specs=[...]
    unnamed x4 -> x3, local copies, waits for them, and re-layouts: 4.66 us -> 3.34 us
where the time goes in v8:
time: 153 us
  Pallas kernels  146 us (95%)
  local copies, waits for them, and re-layouts  4.83 us (3%)
  between operations  1.81 us (1%)
    pallas_call x1, Pallas kernels, local_head(): pl.pallas_call(functools.partial(head_kernel, groups, tokens), in_specs=[...  146 us
    unnamed x3, local copies, waits for them, and re-layouts  3.34 us

profile of v8, /device:TPU:113, one launch (start us, length us, event | category | flops | bytes accessed | tf_op | source)
XLA Modules:
  0.0 152.6 jit_solution(2372346948960150495)
XLA Ops:
  0.6 146.0 %head.1 = (f32[1,128]{1,0:T(1,128)}, f32[5,512,512]{2,1,0:T(8,128)S(1)}, f32[4016,512]{1,0:T(8,128)S(1)}, f32[17,4016,512]{2,1,0:T(8,128)}) custom-call(bf16[2,512,512]{2,1,0:T(8,128)(2,1)} %bitcast.6, s32[4,1,256]{2,1,0:T(1,128)} %bitcast.7, bf16[4016,512]{1,0:T(8,128)(2,1)} %w_hbm.1), custom_call_target="tpu_custom_call" | custom-call | tf_op jit(solution)/shard_map/head/pallas_call | solution.py:403
  146.6 1.5 slice.7
  148.1 0.0 copy-start
  148.1 3.3 %copy.8 = f32[4016,512]{1,0:T(8,128)} copy(f32[4016,512]{1,0:T(8,128)S(1)} %get-tuple-element.11) | data formatting | bytes 16449536
  151.4 0.0 copy-done
Async XLA Ops:
  148.1 3.3 %copy-start = (f32[1,128]{1,0:T(1,128)S(1)}, f32[1,128]{1,0:T(1,128)}, u32[]{:S(2)}) copy-start(f32[1,128]{1,0:T(1,128)} %get-tuple-element.6) | copy-start | bytes 1540

commit v9 on v8

--- a/solution.py
+++ b/solution.py
@@ -324,7 +324,11 @@
         z_load(0, pair_tile(z_next, 1)).start()
         z_load(1, 0).wait()
         bwd_tile(1, pair_tile(pair, 0), 2 + slot, with_dw)
-        z_load(1, pair_tile(z_next, 0)).start()
+
+        @pl.when(pair < last)
+        def _():
+            z_load(1, pair_tile(z_next, 0)).start()
+
         d2d_copy(odd).wait_recv()
 
     def bwd_pair(pair, carry):
@@ -348,7 +352,7 @@
 
     last = len(PAIRS) - 1
     z_load(0, 0).wait()
-    run_pair(jnp.int32(0), 0, 0, False)
+    run_pair(jnp.int32(0), 0, 0, True)
     finish_pair(0)
     lax.fori_loop(1, last + 1, bwd_pair, 0)
 
@@ -362,9 +366,7 @@
 
     for peer in PEERS:
         zt_copy(peer).start()
-    for buf in range(2):
-        z_load(buf, 0).wait()
-        bwd_tile(buf, tile_id("across", 1 - buf, 0))
+    z_load(0, 0).wait()
     finish_pair(last)
     for peer in PEERS:
         zt_copy(peer).wait()

time: 153 us -> 154 us (level)
  Pallas kernels: 146 us -> 148 us
    pallas_call x1, Pallas kernels: 146 us -> 148 us  [local_head(): pl.pallas_call(functools.partial(head_kernel, groups, tokens), in_specs=[...]
where the time goes in v9:
time: 154 us
  Pallas kernels  148 us (96%)
  local copies, waits for them, and re-layouts  4.83 us (3%)
  between operations  1.81 us (1%)
    pallas_call x1, Pallas kernels, local_head(): pl.pallas_call(functools.partial(head_kernel, groups, tokens), in_specs=[...  148 us
    unnamed x3, local copies, waits for them, and re-layouts  3.34 us

profile of v9, /device:TPU:113, one launch (start us, length us, event | category | flops | bytes accessed | tf_op | source)
XLA Modules:
  0.0 154.3 jit_solution(12825224033874660286)
XLA Ops:
  0.6 147.6 %head.1 = (f32[1,128]{1,0:T(1,128)}, f32[5,512,512]{2,1,0:T(8,128)S(1)}, f32[4016,512]{1,0:T(8,128)S(1)}, f32[17,4016,512]{2,1,0:T(8,128)}) custom-call(bf16[2,512,512]{2,1,0:T(8,128)(2,1)} %bitcast.6, s32[4,1,256]{2,1,0:T(1,128)} %bitcast.7, bf16[4016,512]{1,0:T(8,128)(2,1)} %w_hbm.1), custom_call_target="tpu_custom_call" | custom-call | tf_op jit(solution)/shard_map/head/pallas_call | solution.py:405
  148.3 1.5 slice.7
  149.8 0.0 copy-start
  149.8 3.3 %copy.8 = f32[4016,512]{1,0:T(8,128)} copy(f32[4016,512]{1,0:T(8,128)S(1)} %get-tuple-element.11) | data formatting | bytes 16449536
  153.1 0.0 copy-done
Async XLA Ops:
  149.8 3.3 %copy-start = (f32[1,128]{1,0:T(1,128)S(1)}, f32[1,128]{1,0:T(1,128)}, u32[]{:S(2)}) copy-start(f32[1,128]{1,0:T(1,128)} %get-tuple-element.6) | copy-start | bytes 1540
